TPU v7x, 16 devices: a 4x2x1 block of a 4x4x8 slice. The times are simulated.
16 devices in a mesh: dp: 2 (over y, z), sp: 8 (over x, core).
Axes of the slice: x: 4, y: 2, z: 1, core: 2. Of those that a mesh axis runs over, the one named last changes fastest.
The devices are a block of a 4x4x8 slice.
Arguments:
- x_in: bfloat16 [8, 4096, 2304], P('dp', 'sp'), parts along dimension 0
- dy_in: bfloat16 [8, 4096, 2304], P('dp', 'sp'), parts along dimension 0
- positions: int32 [8192], P(('dp', 'sp')), parts along dimension 0
- w_q: bfloat16 [2304, 2048], replicated
- w_k: bfloat16 [2304, 1024], replicated
- w_v: bfloat16 [2304, 1024], replicated
- w_o: bfloat16 [2048, 2304], replicated
- w_pre: float32 [2304], replicated
- w_post: float32 [2304], replicated
- q_norm: float32 [256], replicated
- k_norm: float32 [256], replicated
Outputs:
- output 1: bfloat16 [8, 4096, 2304], P('dp', 'sp'), parts along dimension 0
- output 2: bfloat16 [8, 4096, 2304], P('dp', 'sp'), parts along dimension 0
- output 3: bfloat16 [4608, 2048], P('dp'), parts along dimension 0
- output 4: bfloat16 [4608, 1024], P('dp'), parts along dimension 0
- output 5: bfloat16 [4608, 1024], P('dp'), parts along dimension 0
- output 6: bfloat16 [4096, 2304], P('dp'), parts along dimension 0
- output 7: float32 [4608], P('dp'), parts along dimension 0
- output 8: float32 [4608], P('dp'), parts along dimension 0
- output 9: float32 [512], P('dp'), parts along dimension 0
- output 10: float32 [512], P('dp'), parts along dimension 0
There are 2 independent parts. A program takes and returns all parts, laid end to end along the dimension named above; an argument that names none is the same for every part.
All inputs are finite; a program needn't handle non-finite values.
Results may differ from a plain program's by a relative error of at most 0.02.
Values are sent between devices in bfloat16 or wider.
A program may use at most 768 MiB of HBM per device.

v0:
```python
import functools
import jax
import jax.numpy as jnp
from jax import lax
from jax.sharding import PartitionSpec as P

EPS = 1e-6
ROPE_BASE = 1000000.0
ROPE_SCALE = 8.0
NEG_BIG = -1e30
Q_BLOCK = 1024


def rms_scale(x_f32, weight):
    inv_rms = lax.rsqrt(jnp.mean(x_f32 * x_f32, axis=-1, keepdims=True) + EPS)
    return x_f32 * inv_rms * (1.0 + weight)


def pre_norm(x_f32, weight):
    return rms_scale(x_f32, weight).astype(jnp.bfloat16)


def post_norm(proj, weight):
    return rms_scale(proj.astype(jnp.float32), weight)


def rope_tables(positions, head):
    half_dim = head // 2
    inv_freq = ROPE_BASE ** (-jnp.arange(half_dim, dtype=jnp.float32) * 2.0 / head)
    angles = (positions.astype(jnp.float32) / ROPE_SCALE)[:, None] * inv_freq[None, :]
    return jnp.cos(angles), jnp.sin(angles)


def norm_rope(heads_bf, weight, cosines, sines):
    half_dim = heads_bf.shape[-1] // 2
    normed = rms_scale(heads_bf.astype(jnp.float32), weight)
    first = normed[..., :half_dim]
    second = normed[..., half_dim:]
    cos_b = cosines[None, :, None, :]
    sin_b = sines[None, :, None, :]
    rotated = jnp.concatenate([first * cos_b - second * sin_b, second * cos_b + first * sin_b], axis=-1)
    return rotated.astype(jnp.bfloat16)


def causal_mask(start, block, end):
    row_ids = start + jnp.arange(block)
    col_ids = jnp.arange(end)
    return row_ids[:, None] >= col_ids[None, :]


def attention_fwd(q_all, k_all, v_all):
    batch, seq, q_heads, head = q_all.shape
    kv_loc = k_all.shape[2]
    scale = head ** -0.5
    block = min(Q_BLOCK, seq)
    q_grp = q_all.reshape(batch, seq, kv_loc, q_heads // kv_loc, head)
    pieces = []
    row_lse = []
    for index in range(seq // block):
        start = index * block
        end = start + block
        scores = jnp.einsum('bqkgh,bskh->bkgqs', q_grp[:, start:end], k_all[:, :end], preferred_element_type=jnp.float32) * scale
        scores = jnp.where(causal_mask(start, block, end), scores, NEG_BIG)
        row_max = jnp.max(scores, axis=-1, keepdims=True)
        exp_scores = jnp.exp(scores - row_max)
        row_sum = jnp.sum(exp_scores, axis=-1, keepdims=True)
        attn_prob = (exp_scores / row_sum).astype(jnp.bfloat16)
        pieces.append(jnp.einsum('bkgqs,bskh->bqkgh', attn_prob, v_all[:, :end], preferred_element_type=jnp.float32).astype(jnp.bfloat16))
        row_lse.append(row_max + jnp.log(row_sum))
    return jnp.concatenate(pieces, axis=1).reshape(batch, seq, q_heads, head), row_lse


def attention_bwd(q_all, k_all, v_all, row_lse, d_out):
    batch, seq, q_heads, head = q_all.shape
    kv_loc = k_all.shape[2]
    per_kv = q_heads // kv_loc
    scale = head ** -0.5
    block = min(Q_BLOCK, seq)
    q_grp = q_all.reshape(batch, seq, kv_loc, per_kv, head)
    do_grp = d_out.reshape(batch, seq, kv_loc, per_kv, head)
    dk_acc = jnp.zeros(k_all.shape, jnp.float32)
    dv_acc = jnp.zeros(v_all.shape, jnp.float32)
    dq_pieces = []
    for index in range(seq // block):
        start = index * block
        end = start + block
        q_blk = q_grp[:, start:end]
        do_blk = do_grp[:, start:end]
        k_pre = k_all[:, :end]
        v_pre = v_all[:, :end]
        scores = jnp.einsum('bqkgh,bskh->bkgqs', q_blk, k_pre, preferred_element_type=jnp.float32) * scale
        scores = jnp.where(causal_mask(start, block, end), scores, NEG_BIG)
        attn_prob = jnp.exp(scores - row_lse[index])
        d_prob = jnp.einsum('bqkgh,bskh->bkgqs', do_blk, v_pre, preferred_element_type=jnp.float32)
        d_score = (attn_prob * (d_prob - jnp.sum(d_prob * attn_prob, axis=-1, keepdims=True)) * scale).astype(jnp.bfloat16)
        dq_pieces.append(jnp.einsum('bkgqs,bskh->bqkgh', d_score, k_pre, preferred_element_type=jnp.float32).astype(jnp.bfloat16))
        dk_part = jnp.einsum('bkgqs,bqkgh->bskh', d_score, q_blk, preferred_element_type=jnp.float32)
        dv_part = jnp.einsum('bkgqs,bqkgh->bskh', attn_prob.astype(jnp.bfloat16), do_blk, preferred_element_type=jnp.float32)
        dk_acc = lax.dynamic_update_slice(dk_acc, dk_acc[:, :end] + dk_part, (0, 0, 0, 0))
        dv_acc = lax.dynamic_update_slice(dv_acc, dv_acc[:, :end] + dv_part, (0, 0, 0, 0))
    dq_all = jnp.concatenate(dq_pieces, axis=1).reshape(batch, seq, q_heads, head)
    return dq_all, dk_acc.astype(jnp.bfloat16), dv_acc.astype(jnp.bfloat16)


def fold_copies(grad_wide, kv_heads, rep):
    if rep == 1:
        return grad_wide
    batch, seq_loc, wide, head = grad_wide.shape
    summed = jnp.sum(grad_wide.reshape(batch, seq_loc, kv_heads, rep, head), axis=3, dtype=jnp.float32)
    return summed.astype(jnp.bfloat16)


def solution(mesh):
    group = mesh.shape['sp']

    def to_heads(arr):
        return lax.all_to_all(arr, 'sp', 2, 1, tiled=True)

    def to_tokens(arr):
        return lax.all_to_all(arr, 'sp', 1, 2, tiled=True)

    def device_step(x_in, dy_in, positions, w_q, w_k, w_v, w_o, w_pre, w_post, q_norm, k_norm):
        batch, seq_loc, width = x_in.shape
        head = q_norm.shape[0]
        heads = w_q.shape[1] // head
        kv_heads = w_k.shape[1] // head
        rep = max(1, group // kv_heads)
        x_f32 = x_in.astype(jnp.float32)
        normed, pre_pull = jax.vjp(pre_norm, x_f32, w_pre)
        q_proj = jnp.einsum('bsd,dn->bsn', normed, w_q, preferred_element_type=jnp.float32).astype(jnp.bfloat16).reshape(batch, seq_loc, heads, head)
        k_proj = jnp.einsum('bsd,dn->bsn', normed, w_k, preferred_element_type=jnp.float32).astype(jnp.bfloat16).reshape(batch, seq_loc, kv_heads, head)
        v_proj = jnp.einsum('bsd,dn->bsn', normed, w_v, preferred_element_type=jnp.float32).astype(jnp.bfloat16).reshape(batch, seq_loc, kv_heads, head)
        cosines, sines = rope_tables(positions, head)
        q_rot, q_pull = jax.vjp(functools.partial(norm_rope, cosines=cosines, sines=sines), q_proj, q_norm)
        k_rot, k_pull = jax.vjp(functools.partial(norm_rope, cosines=cosines, sines=sines), k_proj, k_norm)
        q_all = to_heads(q_rot)
        k_all = to_heads(jnp.repeat(k_rot, rep, axis=2))
        v_all = to_heads(jnp.repeat(v_proj, rep, axis=2))
        o_all, row_lse = attention_fwd(q_all, k_all, v_all)
        o_flat = to_tokens(o_all).reshape(batch, seq_loc, heads * head)
        proj = jnp.einsum('bsn,nd->bsd', o_flat, w_o, preferred_element_type=jnp.float32).astype(jnp.bfloat16)
        post, post_pull = jax.vjp(post_norm, proj, w_post)
        y_out = (x_f32 + post).astype(jnp.bfloat16)
        dy_f32 = dy_in.astype(jnp.float32)
        d_proj, dw_post = post_pull(dy_f32)
        dw_o = jnp.einsum('bsn,bsd->nd', o_flat, d_proj, preferred_element_type=jnp.float32)
        d_oflat = jnp.einsum('bsd,nd->bsn', d_proj, w_o, preferred_element_type=jnp.float32).astype(jnp.bfloat16)
        d_oall = to_heads(d_oflat.reshape(batch, seq_loc, heads, head))
        dq_all, dk_all, dv_all = attention_bwd(q_all, k_all, v_all, row_lse, d_oall)
        dq_rot = to_tokens(dq_all)
        dk_rot = fold_copies(to_tokens(dk_all), kv_heads, rep)
        dv_proj = fold_copies(to_tokens(dv_all), kv_heads, rep)
        dq_proj, dq_norm = q_pull(dq_rot)
        dk_proj, dk_norm = k_pull(dk_rot)
        dq_flat = dq_proj.reshape(batch, seq_loc, heads * head)
        dk_flat = dk_proj.reshape(batch, seq_loc, kv_heads * head)
        dv_flat = dv_proj.reshape(batch, seq_loc, kv_heads * head)
        dw_q = jnp.einsum('bsd,bsn->dn', normed, dq_flat, preferred_element_type=jnp.float32)
        dw_k = jnp.einsum('bsd,bsn->dn', normed, dk_flat, preferred_element_type=jnp.float32)
        dw_v = jnp.einsum('bsd,bsn->dn', normed, dv_flat, preferred_element_type=jnp.float32)
        d_normed = (jnp.einsum('bsn,dn->bsd', dq_flat, w_q, preferred_element_type=jnp.float32)
                    + jnp.einsum('bsn,dn->bsd', dk_flat, w_k, preferred_element_type=jnp.float32)
                    + jnp.einsum('bsn,dn->bsd', dv_flat, w_v, preferred_element_type=jnp.float32)).astype(jnp.bfloat16)
        dx_norm, dw_pre = pre_pull(d_normed)
        dx_out = (dy_f32 + dx_norm).astype(jnp.bfloat16)
        sums = lax.psum((dw_q, dw_k, dw_v, dw_o, dw_pre, dw_post, dq_norm, dk_norm), 'sp')
        return (y_out, dx_out, sums[0].astype(jnp.bfloat16), sums[1].astype(jnp.bfloat16), sums[2].astype(jnp.bfloat16), sums[3].astype(jnp.bfloat16), sums[4], sums[5], sums[6], sums[7])

    token_spec = P('dp', 'sp', None)
    return jax.shard_map(device_step, mesh=mesh,
                         in_specs=(token_spec, token_spec, P(('dp', 'sp')), P(None, None), P(None, None), P(None, None), P(None, None), P(None), P(None), P(None), P(None)),
                         out_specs=(token_spec, token_spec, P('dp', None), P('dp', None), P('dp', None), P('dp', None), P('dp'), P('dp'), P('dp'), P('dp')),
                         check_vma=False)
```

profile of v0, /device:TPU:112, one launch (start us, length us, event | category | flops | bytes accessed | tf_op | source)
XLA Modules:
  0.0 2302.7 jit_solution(2529961150078394838)
XLA Ops:
  7.1 14.0 fusion.110
  50.4 16.1 convert_convert_fusion.1
  77.0 13.2 copy.351
  121.5 22.0 all-to-all-done
  150.1 14.0 all-to-all-start.1
  164.1 24.2 %convert_convert_fusion = f32[4,512,2048]{2,1,0:T(8,128)S(1)} fusion(bf16[2304,2048]{1,0:T(8,128)(2,1)} %param.14, bf16[4,512,2304]{2,1,0:T(8,128)(2,1)} %param.11, f32[2304]{0:T(1024)S(1)} %broadcast_add_fusion.1, f32[4,512]{1,0:T(4,128)S(1)} %fusion.130), kind=kOutput, calls=%fused_computation.153 | convolution fusion | flops 19354615808 | bytes 35668992 | tf_op jit(solution)/shard_map/bsd,dn->bsn/dot_general | solution.py:130
  188.3 11.7 copy.471
  234.0 24.2 %all-to-all-done.1 = bf16[4,512,8,256]{3,1,0,2:T(8,128)(2,1)} async-done(((bf16[4,512,8,256]{3,1,0,2:T(8,128)(2,1)}), bf16[4,512,8,256]{3,1,0,2:T(8,128)(2,1)}, u32[]{:S(2)}, u32[]{:S(2)}) %all-to-all-start.1) | async-done | bytes 8388640 | tf_op jit(solution)/shard_map/all_to_all | solution.py:117
  276.6 12.0 copy.349
  288.6 13.4 reshape.507
  317.6 40.2 %all-to-all-done.2 = bf16[4,512,8,256]{3,1,0,2:T(8,128)(2,1)} async-done(((bf16[4,512,8,256]{3,1,0,2:T(8,128)(2,1)}), bf16[4,512,8,256]{3,1,0,2:T(8,128)(2,1)}, u32[]{:S(2)}, u32[]{:S(2)}) %all-to-all-start.2) | async-done | bytes 8388640 | tf_op jit(solution)/shard_map/all_to_all | solution.py:117
  365.4 11.1 fusion.143
  376.5 16.6 fusion.142
  411.9 13.0 fusion.23
  425.0 16.4 convert_bitcast_fusion.7
  441.3 21.6 fusion.141
  463.0 19.5 fusion.10
  482.5 21.1 convert_bitcast_fusion.6
  503.7 28.5 %fusion.140 = (f32[4,1024]{1,0:T(4,128)S(1)}, f32[4,1,1,1024,4096]{3,4,0,2,1:T(8,128)}) fusion(bf16[4,4096,256]{2,1,0:T(8,128)(2,1)} %bitcast.477, bf16[4,4096,1,1,256]{4,1,0,3,2:T(8,128)(2,1)} %bitcast.469, pred[1024,4096]{0,1:T(8,128)(4,1)} %iota_compare_fusion), kind=kOutput, calls=%fused_computation.233 | convolution fusion | flops 8640262144 | bytes 81805312 | tf_op jit(solution)/shard_map/bqkgh,bskh->bkgqs/dot_general | solution.py:62
  532.2 21.3 fusion.4
  553.5 27.6 %convert_bitcast_fusion.5 = bf16[4,1024,1,1,256]{1,4,0,3,2:T(8,128)(2,1)} fusion(bf16[4,4096,256]{1,2,0:T(8,128)(2,1)} %reshape.507, f32[4,1024]{1,0:T(4,128)S(1)} %fusion.4, f32[4,1,1,1024,4096]{3,4,0,2,1:T(8,128)} %get-tuple-element.38, f32[4,1024]{1,0:T(4,128)S(1)} %get-tuple-element.37), kind=kOutput, calls=%fused_computation.200 | convolution fusion | flops 8641314816 | bytes 77627392 | tf_op jit(solution)/shard_map/bkgqs,bskh->bqkgh/dot_general | solution.py:68
  587.6 13.6 copy.366
  606.9 94.4 %all-to-all-done.3 = bf16[4,4096,1,256]{3,0,2,1:T(4,128)(2,1)} async-done(((bf16[4,4096,1,256]{3,0,2,1:T(4,128)(2,1)}), bf16[4,4096,1,256]{3,0,2,1:T(4,128)(2,1)}, u32[]{:S(2)}, u32[]{:S(2)}) %all-to-all-start.3) | async-done | bytes 8388640 | tf_op jit(solution)/shard_map/all_to_all | solution.py:120
  701.2 11.5 copy.479
  712.8 13.6 reshape.512
  726.4 25.0 %fusion.41 = (f32[4,512]{1,0:T(4,128)S(1)}, bf16[4,512,2304]{2,1,0:T(8,128)(2,1)S(1)}) fusion(bf16[4,512,2048]{2,1,0:T(8,128)(2,1)} %reshape.512, bf16[2048,2304]{1,0:T(8,128)(2,1)} %param.17), kind=kOutput, calls=%fused_computation.74 | convolution fusion | flops 19346225152 | bytes 27271168 | tf_op jit(solution)/shard_map/bsn,nd->bsd/dot_general | solution.py:141
  751.5 18.5 fusion.39
  770.0 26.9 %fusion.95 = bf16[4,512,2048]{2,1,0:T(8,128)(2,1)} fusion(bf16[2048,2304]{1,0:T(8,128)(2,1)} %param.17, bf16[4,512,2304]{2,1,0:T(8,128)(2,1)} %param.12, bf16[4,512,2304]{2,1,0:T(8,128)(2,1)} %copy-done.4, f32[4,512]{1,0:T(4,128)S(1)} %multiply_multiply_fusion.4, f32[2304]{0:T(1024)S(1)} %broadcast_add_fusion, f32[4,512]{1,0:T(4,128)S(1)} %fusion.131), kind=kOutput, calls=%fused_computation.163 | convolution fusion | flops 19369295872 | bytes 36725760 | tf_op jit(solution)/shard_map/bsd,nd->bsn/dot_general | solution.py:147
  810.9 30.5 %convolution_bitcast_fusion = f32[2048,2304]{1,0:T(8,128)} fusion(bf16[4,512,2048]{2,1,0:T(8,128)(2,1)} %reshape.512, bf16[4,512,2304]{2,1,0:T(8,128)(2,1)} %param.12, bf16[4,512,2304]{2,1,0:T(8,128)(2,1)} %copy-done.4, f32[4,512]{1,0:T(4,128)S(1)} %multiply_multiply_fusion.4, f32[2304]{0:T(1024)S(1)} %broadcast_add_fusion, f32[4,512]{1,0:T(4,128)S(1)} %fusion.131), kind=kOutput, calls=%fused_computation.113 | convolution fusion | flops 19365101568 | bytes 46162944 | tf_op jit(solution)/shard_map/bsn,bsd->nd/dot_general | solution.py:146
  841.4 63.2 %all-to-all-done.4 = bf16[4,512,8,256]{3,1,0,2:T(8,128)(2,1)} async-done(((bf16[4,512,8,256]{3,1,0,2:T(8,128)(2,1)}), bf16[4,512,8,256]{3,1,0,2:T(8,128)(2,1)}, u32[]{:S(2)}, u32[]{:S(2)}) %all-to-all-start.4) | async-done | bytes 8388640 | tf_op jit(solution)/shard_map/all_to_all | solution.py:117
  912.2 12.0 fusion.115
  924.2 13.2 fusion.55
  937.4 25.2 %fusion.16 = (f32[4,1024]{1,0:T(4,128)}, f32[4,2048,1024]{2,1,0:T(8,128)}) fusion(f32[4,1,1,1024,2048]{3,4,0,2,1:T(8,128)} %get-tuple-element.42, f32[4,1024]{1,0:T(4,128)S(1)} %log_add_fusion.2, bf16[4,4096,1,1,256]{4,1,0,3,2:T(8,128)(2,1)S(1)} %bitcast.452, bf16[4,4096,1,256]{1,3,0,2:T(8,128)(2,1)} %bitcast.459), kind=kOutput, calls=%fused_computation.35 | convolution fusion | flops 4320129024 | bytes 73433088 | tf_op jit(solution)/shard_map/bqkgh,bskh->bkgqs/dot_general | solution.py:94
  972.9 20.4 fusion.81
  993.3 35.3 %fusion.6 = (f32[4,1024]{1,0:T(4,128)}, f32[4,3072,1024]{2,1,0:T(8,128)}) fusion(f32[4,1,1,1024,3072]{3,4,0,2,1:T(8,128)} %get-tuple-element.40, f32[4,1024]{1,0:T(4,128)S(1)} %log_add_fusion.1, bf16[4,4096,1,1,256]{4,1,0,3,2:T(8,128)(2,1)} %bitcast.447, bf16[4,4096,1,256]{1,3,0,2:T(8,128)(2,1)} %bitcast.460), kind=kOutput, calls=%fused_computation.15 | convolution fusion | flops 6480195584 | bytes 109084672 | tf_op jit(solution)/shard_map/bqkgh,bskh->bkgqs/dot_general | solution.py:94
  1028.6 27.7 %fusion.65 = f32[4,4096,1,256]{1,3,0,2:T(8,128)} fusion(f32[4,4096,1,256]{1,3,0,2:T(8,128)} %fusion.81, f32[4,1,1,1024,3072]{3,4,0,2,1:T(8,128)} %get-tuple-element.40, f32[4,1024]{1,0:T(4,128)S(1)} %log_add_fusion.1, bf16[4,4096,1,1,256]{4,1,0,3,2:T(8,128)(2,1)} %bitcast.448), kind=kOutput, calls=%fused_computation.117 | convolution fusion | flops 6470762496 | bytes 77611008 | tf_op jit(solution)/shard_map/bkgqs,bqkgh->bskh/dot_general | solution.py:98
  1056.3 46.5 %fusion = (f32[4,1024]{1,0:T(4,128)S(1)}, f32[4,4096,1024]{2,1,0:T(8,128)}) fusion(f32[4,1,1,1024,4096]{3,4,0,2,1:T(8,128)} %get-tuple-element.38, f32[4,1024]{1,0:T(4,128)S(1)} %copy-done.22, bf16[4,4096,256]{1,2,0:T(8,128)(2,1)} %reshape.507, bf16[4,4096,1,1,256]{4,1,0,3,2:T(8,128)(2,1)} %bitcast.449), kind=kOutput, calls=%fused_computation.3 | convolution fusion | flops 8640262144 | bytes 144736256 | tf_op jit(solution)/shard_map/bqkgh,bskh->bkgqs/dot_general | solution.py:94
  1102.8 31.4 %fusion.53 = bf16[4,4096,1,256]{1,3,0,2:T(8,128)(2,1)} fusion(f32[4,4096,1,256]{1,3,0,2:T(8,128)} %fusion.65, f32[4,1,1,1024,4096]{3,4,0,2,1:T(8,128)} %get-tuple-element.38, f32[4,1024]{1,0:T(4,128)S(1)} %copy-done.22, bf16[4,4096,1,1,256]{4,1,0,3,2:T(8,128)(2,1)} %bitcast.450), kind=kOutput, calls=%fused_computation.91 | convolution fusion | flops 8631877632 | bytes 94388224 | tf_op jit(solution)/shard_map/bkgqs,bqkgh->bskh/dot_general | solution.py:98
  1134.2 13.6 copy.410
  1153.3 11.9 fusion.80
  1180.7 28.2 %fusion.50 = bf16[4,1024,2048]{1,2,0:T(8,128)(2,1)} fusion(f32[4,2048,1024]{2,1,0:T(8,128)} %get-tuple-element.50, f32[4,1,1,1024,2048]{3,4,0,2,1:T(8,128)} %get-tuple-element.42, f32[4,1024]{1,0:T(4,128)S(1)} %copy-done.36, f32[4,1024]{1,0:T(4,128)S(1)} %copy-done.16), kind=kLoop, calls=%fused_computation.83 | loop fusion | flops 41943040 | bytes 83918848 | tf_op jit(solution)/shard_map/reshape.85
  1208.9 13.4 fusion.82
  1222.3 40.8 %fusion.28 = bf16[4,1024,3072]{1,2,0:T(8,128)(2,1)} fusion(f32[4,3072,1024]{2,1,0:T(8,128)} %get-tuple-element.52, f32[4,1,1,1024,3072]{3,4,0,2,1:T(8,128)} %get-tuple-element.40, f32[4,1024]{1,0:T(4,128)S(1)} %copy-done.35, f32[4,1024]{1,0:T(4,128)S(1)} %log_add_fusion.1), kind=kLoop, calls=%fused_computation.58 | loop fusion | flops 62914560 | bytes 125861888 | tf_op jit(solution)/shard_map/reshape.93
  1263.1 53.5 %fusion.15 = bf16[4,1024,4096]{1,2,0:T(8,128)(2,1)} fusion(f32[4,4096,1024]{2,1,0:T(8,128)} %get-tuple-element.54, f32[4,1,1,1024,4096]{3,4,0,2,1:T(8,128)} %get-tuple-element.38, f32[4,1024]{1,0:T(4,128)S(1)} %get-tuple-element.53, f32[4,1024]{1,0:T(4,128)S(1)} %copy-done.22), kind=kLoop, calls=%fused_computation.31 | loop fusion | flops 83886080 | bytes 167804928 | tf_op jit(solution)/shard_map/reshape.101
  1316.7 20.6 fusion.66
  1337.2 21.5 fusion.54
  1358.7 13.6 copy.396
  1372.3 16.4 convert_bitcast_fusion.2
  1401.9 12.9 convert_bitcast_fusion.3
  1414.8 22.4 convert_bitcast_fusion.1
  1443.7 13.8 copy.382
  1457.5 12.4 reduce_sum.252
  1477.3 16.8 convolution_bitcast_fusion.2
  1499.6 12.4 reduce_sum.250
  1546.2 15.8 fusion.102
  1562.0 15.5 fusion.98
  1577.4 13.6 convolution_bitcast_fusion.3
  1601.9 11.3 convert_bitcast_fusion
  1622.8 11.5 multiply_reduce_fusion
  1644.1 11.3 copy.386
  1655.5 28.6 %convolution_bitcast_fusion.1 = f32[2304,2048]{1,0:T(8,128)} fusion(bf16[4,512,2048]{1,2,0:T(8,128)(2,1)} %bitcast.482, bf16[4,512,2304]{2,1,0:T(8,128)(2,1)} %param.11, f32[2304]{0:T(1024)S(1)} %copy-done.47, f32[4,512]{1,0:T(4,128)S(1)} %copy-done.50), kind=kOutput, calls=%fused_computation.114 | convolution fusion | flops 19346227200 | bytes 36717568 | tf_op jit(solution)/shard_map/bsd,bsn->dn/dot_general | solution.py:158
  1684.0 36.9 %fusion.37 = (f32[2304]{0:T(1024)S(1)}, f32[4,512]{1,0:T(4,128)S(1)}, bf16[4,512,2304]{2,1,0:T(8,128)(2,1)}) fusion(bf16[4,512,2304]{2,1,0:T(8,128)(2,1)} %param.11, f32[4,512]{1,0:T(4,128)S(1)} %copy-done.50, f32[2304]{0:T(1024)S(1)} %copy-done.47, f32[4,512,2304]{2,1,0:T(8,128)} %fusion.102, f32[4,512,2304]{2,1,0:T(8,128)} %fusion.98, ...), kind=kOutput, calls=%fused_computation.70 | convolution fusion | flops 19379253248 | bytes 74483712 | tf_op jit(solution)/shard_map/bsn,dn->bsd/dot_general | solution.py:161
  1721.0 16.1 fusion.38
  1737.1 565.2 %all-reduce.8 = (bf16[2304,2048]{1,0:T(8,128)(2,1)}, bf16[2304,1024]{1,0:T(8,128)(2,1)}, bf16[2304,1024]{1,0:T(8,128)(2,1)}, bf16[2048,2304]{1,0:T(8,128)(2,1)},...) all-reduce(f32[2304,2048]{1,0:T(8,128)} %convolution_bitcast_fusion, ...), channel_id=1, replica_groups=mesh['dp'=2,'sp'=8] {'sp'}, use_global_device_ids=true, to_apply=%region_22.23 | all-reduce | flops 14160896 | bytes 84975616 | tf_op jit(solution)/shard_map/psum | solution.py:166
  (229 shorter events, 339.9 us)
Async XLA Ops:
  0.6 6.4 copy-start.1
  0.7 6.4 copy-start.55
  7.0 157.1 %copy-start.49 = (f32[4,512]{1,0:T(4,128)}, f32[4,512]{1,0:T(4,128)S(1)}, u32[]{:S(2)}) copy-start(f32[4,512]{1,0:T(4,128)S(1)} %fusion.130) | copy-start | bytes 24580
  7.1 157.0 %copy-start.46 = (f32[2304]{0:T(1024)}, f32[2304]{0:T(1024)S(1)}, u32[]{:S(2)}) copy-start(f32[2304]{0:T(1024)S(1)} %broadcast_add_fusion.1) | copy-start | bytes 27652
  43.3 100.3 %all-to-all-start = ((bf16[4,512,8,256]{1,3,0,2:T(8,128)(2,1)}), bf16[4,512,8,256]{1,3,0,2:T(8,128)(2,1)}, u32[]{:S(2)}, u32[]{:S(2)}) async-start(bf16[4,512,8,256]{1,3,0,2:T(8,128)(2,1)} %bitcast.462), calls=%async_computation | async-start | bytes 16777216 | tf_op jit(solution)/shard_map/all_to_all | solution.py:117
  50.1 54.6 %copy-start.5 = (f32[512,128]{0,1:T(8,128)}, f32[512,128]{0,1:T(8,128)S(1)}, u32[]{:S(2)}) copy-start(f32[512,128]{0,1:T(8,128)S(1)} %get-tuple-element.35) | copy-start | bytes 786436
  50.1 54.6 %copy-start.7 = (f32[512,128]{0,1:T(8,128)}, f32[512,128]{0,1:T(8,128)S(1)}, u32[]{:S(2)}) copy-start(f32[512,128]{0,1:T(8,128)S(1)} %get-tuple-element.36) | copy-start | bytes 786436
  50.3 166.0 %copy-start.10 = (f32[512,128]{1,0:T(8,128)}, f32[512,128]{1,0:T(8,128)S(1)}, u32[]{:S(2)}) copy-start(f32[512,128]{1,0:T(8,128)S(1)} %copy.356) | copy-start | bytes 786436
  50.4 165.8 %copy-start.12 = (f32[512,128]{1,0:T(8,128)}, f32[512,128]{1,0:T(8,128)S(1)}, u32[]{:S(2)}) copy-start(f32[512,128]{1,0:T(8,128)S(1)} %copy.357) | copy-start | bytes 786436
  96.3 13.1 copy-start.27
  96.3 13.1 copy-start.53
  96.3 13.0 copy-start.25
  150.1 108.1 %all-to-all-start.1 = ((bf16[4,512,8,256]{3,1,0,2:T(8,128)(2,1)}), bf16[4,512,8,256]{3,1,0,2:T(8,128)(2,1)}, u32[]{:S(2)}, u32[]{:S(2)}) async-start(bf16[4,512,8,256]{3,1,0,2:T(8,128)(2,1)} %bitcast.463), calls=%async_computation.1 | async-start | bytes 16777216 | tf_op jit(solution)/shard_map/all_to_all | solution.py:117
  188.3 11.7 copy-start
  200.0 8.4 copy-start.60
  208.4 7.9 copy-start.23
  208.4 7.9 copy-start.51
  208.4 7.9 copy-start.17
  258.2 99.5 %all-to-all-start.2 = ((bf16[4,512,8,256]{3,1,0,2:T(8,128)(2,1)}), bf16[4,512,8,256]{3,1,0,2:T(8,128)(2,1)}, u32[]{:S(2)}, u32[]{:S(2)}) async-start(bf16[4,512,8,256]{3,1,0,2:T(8,128)(2,1)} %copy.358), calls=%async_computation.2 | async-start | bytes 16777216 | tf_op jit(solution)/shard_map/all_to_all | solution.py:117
  357.8 7.6 copy-start.19
  376.5 24.6 %copy-start.42 = (f32[4,1024]{1,0:T(4,128)}, f32[4,1024]{1,0:T(4,128)S(1)}, u32[]{:S(2)}) copy-start(f32[4,1024]{1,0:T(4,128)S(1)} %get-tuple-element.43) | copy-start | bytes 49156
  393.1 31.9 %copy-start.31 = (f32[4,1024]{1,0:T(4,128)}, f32[4,1024]{1,0:T(4,128)S(1)}, u32[]{:S(2)}) copy-start(f32[4,1024]{1,0:T(4,128)S(1)} %get-tuple-element.41) | copy-start | bytes 49156
  401.0 10.9 copy-start.44
  425.0 16.4 copy-start.33
  463.0 19.5 copy-start.38
  482.5 21.1 copy-start.40
  553.5 27.6 %copy-start.14 = (bf16[4,1024,1,1,256]{1,4,0,3,2:T(8,128)(2,1)S(1)}, bf16[4,1024,1,1,256]{1,4,0,3,2:T(8,128)(2,1)}, u32[]{:S(2)}) copy-start(bf16[4,1024,1,1,256]{1,4,0,3,2:T(8,128)(2,1)} %convert_bitcast_fusion.8) | copy-start | bytes 6291460
  601.2 100.1 %all-to-all-start.3 = ((bf16[4,4096,1,256]{3,0,2,1:T(4,128)(2,1)}), bf16[4,4096,1,256]{3,0,2,1:T(4,128)(2,1)}, u32[]{:S(2)}, u32[]{:S(2)}) async-start(bf16[4,4096,1,256]{3,0,2,1:T(4,128)(2,1)} %copy.366), calls=%async_computation.3 | async-start | bytes 16777216 | tf_op jit(solution)/shard_map/all_to_all | solution.py:120
  712.8 38.6 %slice-start.6 = ((s8[9437184]{0:T(1024)(128)(4,1)}), s8[1048576]{0:T(1024)(128)(4,1)S(1)}, s32[]{:S(2)}) async-start(s8[9437184]{0:T(1024)(128)(4,1)} %bitcast.442), calls=%async_computation.14 | async-start | bytes 2097152
  726.3 25.1 %slice-start.7 = ((s8[9437184]{0:T(1024)(128)(4,1)}), s8[4194304]{0:T(1024)(128)(4,1)S(1)}, s32[]{:S(2)}) async-start(s8[9437184]{0:T(1024)(128)(4,1)} %bitcast.442), calls=%async_computation.15 | async-start | bytes 8388608
  726.3 25.1 %slice-start.8 = ((s8[9437184]{0:T(1024)(128)(4,1)}), s8[4194304]{0:T(1024)(128)(4,1)S(1)}, s32[]{:S(2)}) async-start(s8[9437184]{0:T(1024)(128)(4,1)} %bitcast.442), calls=%async_computation.16 | async-start | bytes 8388608
  751.4 18.6 copy-start.4
  804.6 99.9 %all-to-all-start.4 = ((bf16[4,512,8,256]{3,1,0,2:T(8,128)(2,1)}), bf16[4,512,8,256]{3,1,0,2:T(8,128)(2,1)}, u32[]{:S(2)}, u32[]{:S(2)}) async-start(bf16[4,512,8,256]{3,1,0,2:T(8,128)(2,1)} %bitcast.464), calls=%async_computation.4 | async-start | bytes 16777216 | tf_op jit(solution)/shard_map/all_to_all | solution.py:117
  810.2 114.0 %copy-start.20 = (f32[4,1024]{1,0:T(4,128)}, f32[4,1024]{1,0:T(4,128)S(1)}, u32[]{:S(2)}) copy-start(f32[4,1024]{1,0:T(4,128)S(1)} %log_add_fusion.3) | copy-start | bytes 49156
  810.2 162.6 %copy-start.15 = (f32[4,1024]{1,0:T(4,128)}, f32[4,1024]{1,0:T(4,128)S(1)}, u32[]{:S(2)}) copy-start(f32[4,1024]{1,0:T(4,128)S(1)} %log_add_fusion.2) | copy-start | bytes 49156
  912.2 12.1 copy-start.2
  1028.6 27.7 %copy-start.22 = (f32[4,1024]{1,0:T(4,128)S(1)}, f32[4,1024]{1,0:T(4,128)}, u32[]{:S(2)}) copy-start(f32[4,1024]{1,0:T(4,128)} %log_add_fusion) | copy-start | bytes 49156
  1147.8 241.0 %all-to-all-start.7 = ((bf16[4,4096,1,256]{3,0,2,1:T(4,128)(2,1)}), bf16[4,4096,1,256]{3,0,2,1:T(4,128)(2,1)}, u32[]{:S(2)}, u32[]{:S(2)}) async-start(bf16[4,4096,1,256]{3,0,2,1:T(4,128)(2,1)} %copy.410), calls=%async_computation.7 | async-start | bytes 16777216 | tf_op jit(solution)/shard_map/all_to_all | solution.py:120
  1172.9 7.8 copy-start.16
  1172.9 7.8 copy-start.36
  1208.9 13.4 copy-start.35
  1388.8 105.2 %all-to-all-start.6 = ((bf16[4,4096,1,256]{3,0,2,1:T(4,128)(2,1)}), bf16[4,4096,1,256]{3,0,2,1:T(4,128)(2,1)}, u32[]{:S(2)}, u32[]{:S(2)}) async-start(bf16[4,4096,1,256]{3,0,2,1:T(4,128)(2,1)} %copy.396), calls=%async_computation.6 | async-start | bytes 16777216 | tf_op jit(solution)/shard_map/all_to_all | solution.py:120
  1457.5 19.8 copy-start.47
  1457.5 19.8 copy-start.50
  1494.0 100.0 %all-to-all-start.5 = ((bf16[4,4096,1,256]{3,0,2,1:T(4,128)(2,1)}), bf16[4,4096,1,256]{3,0,2,1:T(4,128)(2,1)}, u32[]{:S(2)}, u32[]{:S(2)}) async-start(bf16[4,4096,1,256]{3,0,2,1:T(4,128)(2,1)} %copy.382), calls=%async_computation.5 | async-start | bytes 16777216 | tf_op jit(solution)/shard_map/all_to_all | solution.py:120
  1512.0 11.6 copy-start.6
  1512.0 11.6 copy-start.8
  1525.9 11.1 copy-start.28
  1537.0 9.1 copy-start.9
  1546.2 31.3 %slice-start.9 = ((s8[9437184]{0:T(1024)(128)(4,1)}), s8[4194304]{0:T(1024)(128)(4,1)S(1)}, s32[]{:S(2)}) async-start(s8[9437184]{0:T(1024)(128)(4,1)} %bitcast.444), calls=%async_computation.17 | async-start | bytes 8388608
  1546.2 31.3 %slice-start.10 = ((s8[9437184]{0:T(1024)(128)(4,1)}), s8[4194304]{0:T(1024)(128)(4,1)S(1)}, s32[]{:S(2)}) async-start(s8[9437184]{0:T(1024)(128)(4,1)} %bitcast.444), calls=%async_computation.18 | async-start | bytes 8388608
  1562.0 15.5 slice-start.11
  1601.9 11.4 copy-start.11
  1601.9 11.4 copy-start.13
  1613.2 9.6 copy-start.18
  1613.2 9.6 copy-start.52
  1622.8 11.6 slice-start
  1622.8 11.5 copy-start.24
  1622.8 11.6 slice-start.1
  1622.8 11.9 slice-start.2
  1622.8 13.1 slice-start.3
  1684.0 36.9 %copy-start.30 = (f32[4,512]{1,0:T(4,128)S(1)}, f32[4,512]{1,0:T(4,128)}, u32[]{:S(2)}) copy-start(f32[4,512]{1,0:T(4,128)} %copy-done.29) | copy-start | bytes 24580
  1720.9 16.1 copy-start.48
  1721.0 16.1 copy-start.57
  (17 other events, 78.4 us)
where the time goes:
time: 2310 us; the launch traced here: 2300 us
  matrix products  749 us (32%)
  blocking collectives  565 us (24%)
  other arithmetic  404 us (17%)
  local copies, waits for them, and re-layouts  283 us (12%)
  waiting for transfers between devices  247 us (11%)
  starting transfers between devices  52.7 us (2%)
    psum x1, blocking collectives, device_step(): lax.psum((dw_q, dw_k, dw_v, dw_o, dw_pre, dw_post, dq_norm, dk_norm), 'sp')  565 us
    all_to_all x4, waiting for transfers between devices, to_heads(): return lax.all_to_all(arr, 'sp', 2, 1, tiled=True)  150 us
    another operation x6, other arithmetic  143 us
    dot_general x4, matrix products, attention_bwd(): jnp.einsum('bqkgh,bskh->bkgqs', do_blk, v_pre, preferred_element_type=jnp...  120 us
    all_to_all x4, waiting for transfers between devices, to_tokens(): return lax.all_to_all(arr, 'sp', 1, 2, tiled=True)  97.3 us
    dot_general x4, matrix products, attention_bwd(): jnp.einsum('bkgqs,bqkgh->bskh', attn_prob.astype(jnp.bfloat16), do_blk, p...  91.5 us
    dot_general x4, matrix products, attention_fwd(): jnp.einsum('bqkgh,bskh->bkgqs', q_grp[:, start:end], k_all[:, :end], pref...  77.8 us
    dot_general x4, matrix products, attention_fwd(): jnp.einsum('bkgqs,bskh->bqkgh', attn_prob, v_all[:, :end], preferred_elem...  75.9 us
  transfers between devices with their start and end apart: 8, of which 6 were waited for; matrix products, arithmetic and copies ran while one was open for 28% of the time, Pallas kernels for 0%

commit v1 on v0

v1 whole, which is shorter than its diff:
```python
import functools
import jax
import jax.numpy as jnp
from jax import lax
from jax.experimental import pallas as pl
from jax.experimental.pallas import tpu as pltpu
from jax.sharding import PartitionSpec as P

EPS = 1e-6
ROPE_BASE = 1000000.0
ROPE_SCALE = 8.0
NEG_BIG = -1e30
VMEM_LIMIT = 56 * 1024 * 1024
F32 = jnp.float32
BF16 = jnp.bfloat16


def rms_scale(x_f32, weight):
    inv_rms = lax.rsqrt(jnp.mean(x_f32 * x_f32, axis=-1, keepdims=True) + EPS)
    return x_f32 * inv_rms * (1.0 + weight)


def pre_norm(x_f32, weight):
    return rms_scale(x_f32, weight).astype(BF16)


def post_norm(proj, weight):
    return rms_scale(proj.astype(F32), weight)


def rope_tables(positions, head):
    half_dim = head // 2
    inv_freq = ROPE_BASE ** (-jnp.arange(half_dim, dtype=F32) * 2.0 / head)
    angles = (positions.astype(F32) / ROPE_SCALE)[:, None] * inv_freq[None, :]
    return jnp.cos(angles), jnp.sin(angles)


def params(ndim):
    return pltpu.CompilerParams(dimension_semantics=("arbitrary",) * ndim, vmem_limit_bytes=VMEM_LIMIT)


def cost(flops, nbytes):
    return pl.CostEstimate(flops=int(flops), bytes_accessed=int(nbytes), transcendentals=0)


def rotate(x, scale1, cosines, sines):
    half = x.shape[-1] // 2
    inv = lax.rsqrt(jnp.mean(x * x, axis=-1, keepdims=True) + EPS)
    normed = x * inv * scale1
    first, second = normed[:, :half], normed[:, half:]
    return jnp.concatenate([first * cosines - second * sines, second * cosines + first * sines], axis=-1)


def unrotate(dy, x, scale1, cosines, sines):
    half = x.shape[-1] // 2
    inv = lax.rsqrt(jnp.mean(x * x, axis=-1, keepdims=True) + EPS)
    unit = x * inv
    d1, d2 = dy[:, :half], dy[:, half:]
    dn = jnp.concatenate([d1 * cosines + d2 * sines, d2 * cosines - d1 * sines], axis=-1)
    du = dn * scale1
    dx = inv * (du - unit * jnp.mean(du * unit, axis=-1, keepdims=True))
    return dx, jnp.sum(dn * unit, axis=0, keepdims=True)


def packed_spec(tokens, lanes, rep, part, offset=0):
    return pl.BlockSpec((None, None, tokens, lanes), lambda k, b: (k * rep + b // part, b % part, 0, offset))


def flat_spec(tokens, lanes, offset=0):
    return pl.BlockSpec((None, tokens, lanes), lambda k, b: (b, 0, k + offset))


def whole_spec(shape):
    return pl.BlockSpec(shape, lambda k, b: (0,) * len(shape))


def q_pack(q_proj, norm, cosines, sines, head, kv_heads, rep):
    batch, tokens, wide = q_proj.shape
    lanes = wide // kv_heads
    part = batch // rep

    def body(x_ref, w_ref, c_ref, s_ref, o_ref):
        for g in range(lanes // head):
            cols = slice(g * head, (g + 1) * head)
            out = rotate(x_ref[:, cols].astype(F32), 1.0 + w_ref[...], c_ref[...], s_ref[...]).astype(BF16)
            o_ref[:, cols] = (out.astype(F32) * head ** -0.5).astype(BF16)

    return pl.pallas_call(
        body, grid=(kv_heads, batch),
        in_specs=[flat_spec(tokens, lanes), whole_spec((1, head)), whole_spec(cosines.shape), whole_spec(sines.shape)],
        out_specs=packed_spec(tokens, lanes, rep, part),
        out_shape=jax.ShapeDtypeStruct((kv_heads * rep, part, tokens, lanes), BF16),
        compiler_params=params(2), cost_estimate=cost(20 * q_proj.size, 4 * q_proj.size), name='q_pack',
    )(q_proj, norm.reshape(1, head), cosines, sines)


def kv_pack(kv_proj, norm, cosines, sines, head, kv_heads, rep):
    batch, tokens, _ = kv_proj.shape
    part = batch // rep

    def body(k_ref, v_ref, w_ref, c_ref, s_ref, o_ref):
        o_ref[:, :head] = rotate(k_ref[...].astype(F32), 1.0 + w_ref[...], c_ref[...], s_ref[...]).astype(BF16)
        o_ref[:, head:] = v_ref[...]

    return pl.pallas_call(
        body, grid=(kv_heads, batch),
        in_specs=[flat_spec(tokens, head), flat_spec(tokens, head, kv_heads), whole_spec((1, head)),
                  whole_spec(cosines.shape), whole_spec(sines.shape)],
        out_specs=packed_spec(tokens, 2 * head, rep, part),
        out_shape=jax.ShapeDtypeStruct((kv_heads * rep, part, tokens, 2 * head), BF16),
        compiler_params=params(2), cost_estimate=cost(10 * kv_proj.size, 4 * kv_proj.size), name='kv_pack',
    )(kv_proj, kv_proj, norm.reshape(1, head), cosines, sines)


def copy_body(i_ref, o_ref):
    o_ref[...] = i_ref[...]


def pack(flat, kv_heads, rep):
    batch, tokens, wide = flat.shape
    lanes = wide // kv_heads
    part = batch // rep
    return pl.pallas_call(
        copy_body, grid=(kv_heads, batch),
        in_specs=[flat_spec(tokens, lanes)], out_specs=packed_spec(tokens, lanes, rep, part),
        out_shape=jax.ShapeDtypeStruct((kv_heads * rep, part, tokens, lanes), flat.dtype),
        compiler_params=params(2), cost_estimate=cost(2 * flat.size, 4 * flat.size), name='pack',
    )(flat)


def unpack(packed, kv_heads, rep):
    _, part, tokens, lanes = packed.shape
    batch = part * rep
    return pl.pallas_call(
        copy_body, grid=(kv_heads, batch),
        in_specs=[packed_spec(tokens, lanes, rep, part)], out_specs=flat_spec(tokens, lanes),
        out_shape=jax.ShapeDtypeStruct((batch, tokens, kv_heads * lanes), packed.dtype),
        compiler_params=params(2), cost_estimate=cost(2 * packed.size, 4 * packed.size), name='unpack',
    )(packed)


def first_step():
    return jnp.logical_and(pl.program_id(0) == 0, pl.program_id(1) == 0)


def q_unpack(dq, q_proj, norm, cosines, sines, head, kv_heads, rep):
    batch, tokens, wide = q_proj.shape
    lanes = wide // kv_heads
    part = batch // rep

    def body(d_ref, x_ref, w_ref, c_ref, s_ref, o_ref, n_ref):
        @pl.when(first_step())
        def _():
            n_ref[...] = jnp.zeros_like(n_ref)
        for g in range(lanes // head):
            cols = slice(g * head, (g + 1) * head)
            dx, dn = unrotate(d_ref[:, cols].astype(F32), x_ref[:, cols].astype(F32), 1.0 + w_ref[...], c_ref[...], s_ref[...])
            o_ref[:, cols] = dx.astype(BF16)
            n_ref[...] += dn

    return pl.pallas_call(
        body, grid=(kv_heads, batch),
        in_specs=[packed_spec(tokens, lanes, rep, part), flat_spec(tokens, lanes), whole_spec((1, head)),
                  whole_spec(cosines.shape), whole_spec(sines.shape)],
        out_specs=(flat_spec(tokens, lanes), whole_spec((1, head))),
        out_shape=(jax.ShapeDtypeStruct(q_proj.shape, BF16), jax.ShapeDtypeStruct((1, head), F32)),
        compiler_params=params(2), cost_estimate=cost(30 * q_proj.size, 6 * q_proj.size), name='q_unpack',
    )(dq, q_proj, norm.reshape(1, head), cosines, sines)


def kv_unpack(dkv, kv_proj, norm, cosines, sines, head, kv_heads, rep):
    batch, tokens, wide = kv_proj.shape
    part = batch // rep

    def body(d_ref, x_ref, w_ref, c_ref, s_ref, k_ref, v_ref, n_ref):
        @pl.when(first_step())
        def _():
            n_ref[...] = jnp.zeros_like(n_ref)
        dx, dn = unrotate(d_ref[:, :head].astype(F32), x_ref[...].astype(F32), 1.0 + w_ref[...], c_ref[...], s_ref[...])
        k_ref[...] = dx.astype(BF16)
        v_ref[...] = d_ref[:, head:]
        n_ref[...] += dn

    half = jax.ShapeDtypeStruct((batch, tokens, wide // 2), BF16)
    return pl.pallas_call(
        body, grid=(kv_heads, batch),
        in_specs=[packed_spec(tokens, 2 * head, rep, part, 1), flat_spec(tokens, head), whole_spec((1, head)),
                  whole_spec(cosines.shape), whole_spec(sines.shape)],
        out_specs=(flat_spec(tokens, head), flat_spec(tokens, head), whole_spec((1, head))),
        out_shape=(half, half, jax.ShapeDtypeStruct((1, head), F32)),
        compiler_params=params(2), cost_estimate=cost(15 * kv_proj.size, 6 * kv_proj.size), name='kv_unpack',
    )(dkv, kv_proj, norm.reshape(1, head), cosines, sines)


NT = (((1,), (1,)), ((), ()))
TN = (((0,), (0,)), ((), ()))
NN = (((1,), (0,)), ((), ()))


def dot(a, b, dims):
    return lax.dot_general(a, b, dims, preferred_element_type=F32)


def to_row(column):
    return jnp.broadcast_to(column, (column.shape[0], 128)).T[:8, :]


def attention_fwd(q, kv, head):
    slots, part, tokens, lanes = q.shape
    per_kv = lanes // head

    def body(q_ref, kv_ref, o_ref, lse_ref, m_sc, l_sc, acc_sc):
        qi = pl.program_id(1)
        m_sc[...] = jnp.full_like(m_sc, NEG_BIG)
        l_sc[...] = jnp.zeros_like(l_sc)
        acc_sc[...] = jnp.zeros_like(acc_sc)

        def step(kj, masked):
            k = kv_ref[kj, :, :head]
            v = kv_ref[kj, :, head:]
            for g in range(per_kv):
                s = dot(q_ref[:, g * head:(g + 1) * head], k, NT)
                if masked:
                    rows = lax.broadcasted_iota(jnp.int32, s.shape, 0)
                    cols = lax.broadcasted_iota(jnp.int32, s.shape, 1)
                    s = jnp.where(rows >= cols, s, NEG_BIG)
                m_old = m_sc[g]
                m_new = jnp.maximum(m_old, jnp.max(s, axis=-1, keepdims=True))
                p = jnp.exp(s - m_new[:, :1])
                fade = jnp.exp(m_old - m_new)
                l_sc[g] = l_sc[g] * fade + jnp.sum(p, axis=-1, keepdims=True)
                acc_sc[g] = acc_sc[g] * fade[:, :1] + dot(p.astype(BF16), v, NN)
                m_sc[g] = m_new

        def loop_body(kj, carry):
            step(kj, False)
            return carry

        lax.fori_loop(0, qi, loop_body, 0)
        step(qi, True)
        for g in range(per_kv):
            o_ref[:, g * head:(g + 1) * head] = (acc_sc[g] / l_sc[g][:, :1]).astype(BF16)
            lse_ref[g * 8:(g + 1) * 8, :] = (m_sc[g] + jnp.log(l_sc[g])).T[:8, :]

    pairs = part * per_kv * (slots * tokens) ** 2 // 2
    return pl.pallas_call(
        body, grid=(part, slots),
        in_specs=[pl.BlockSpec((None, None, tokens, lanes), lambda b, i: (i, b, 0, 0)),
                  pl.BlockSpec((slots, None, tokens, 2 * head), lambda b, i: (0, b, 0, 0))],
        out_specs=(pl.BlockSpec((None, None, tokens, lanes), lambda b, i: (i, b, 0, 0)),
                   pl.BlockSpec((None, None, per_kv * 8, tokens), lambda b, i: (i, b, 0, 0))),
        out_shape=(jax.ShapeDtypeStruct(q.shape, BF16), jax.ShapeDtypeStruct((slots, part, per_kv * 8, tokens), F32)),
        scratch_shapes=[pltpu.VMEM((per_kv, tokens, 128), F32), pltpu.VMEM((per_kv, tokens, 128), F32),
                        pltpu.VMEM((per_kv, tokens, head), F32)],
        compiler_params=params(2), cost_estimate=cost(8 * pairs * head, 8 * q.size), name='attention_fwd',
    )(q, kv)


def row_dots(o, d_o, head):
    slots, part, tokens, lanes = o.shape
    per_kv = lanes // head

    def body(o_ref, d_ref, out_ref):
        for g in range(per_kv):
            cols = slice(g * head, (g + 1) * head)
            total = jnp.sum(o_ref[:, cols].astype(F32) * d_ref[:, cols].astype(F32), axis=-1, keepdims=True)
            out_ref[g * 8:(g + 1) * 8, :] = to_row(total)

    spec = pl.BlockSpec((None, None, tokens, lanes), lambda b, i: (i, b, 0, 0))
    return pl.pallas_call(
        body, grid=(part, slots), in_specs=[spec, spec],
        out_specs=pl.BlockSpec((None, None, per_kv * 8, tokens), lambda b, i: (i, b, 0, 0)),
        out_shape=jax.ShapeDtypeStruct((slots, part, per_kv * 8, tokens), F32),
        compiler_params=params(2), cost_estimate=cost(4 * o.size, 4 * o.size), name='row_dots',
    )(o, d_o)


def attention_bwd(q, kv, d_o, lse, delta, head):
    slots, part, tokens, lanes = q.shape
    per_kv = lanes // head

    def body(q_ref, kv_ref, d_ref, lse_ref, delta_ref, out_ref, dq_sc, dk_sc, dv_sc):
        kj = pl.program_id(1)
        dk_sc[...] = jnp.zeros_like(dk_sc)
        dv_sc[...] = jnp.zeros_like(dv_sc)

        @pl.when(kj == 0)
        def _():
            dq_sc[...] = jnp.zeros_like(dq_sc)

        def step(qi, masked):
            k = kv_ref[:, :head]
            v = kv_ref[:, head:]
            for g in range(per_kv):
                cols = slice(g * head, (g + 1) * head)
                q_g = q_ref[qi, :, cols]
                d_g = d_ref[qi, :, cols]
                s = dot(k, q_g, NT)
                if masked:
                    key_ids = lax.broadcasted_iota(jnp.int32, s.shape, 0)
                    row_ids = lax.broadcasted_iota(jnp.int32, s.shape, 1)
                    s = jnp.where(row_ids >= key_ids, s, NEG_BIG)
                p = jnp.exp(s - lse_ref[qi, g * 8:g * 8 + 1, :])
                dp = dot(v, d_g, NT)
                ds = (p * (dp - delta_ref[qi, g * 8:g * 8 + 1, :])).astype(BF16)
                dv_sc[...] += dot(p.astype(BF16), d_g, NN)
                dk_sc[...] += dot(ds, q_g, NN)
                dq_sc[qi, :, cols] += dot(ds, k, TN)

        def loop_body(qi, carry):
            step(qi, False)
            return carry

        step(kj, True)
        lax.fori_loop(kj + 1, slots, loop_body, 0)
        out_ref[:, :lanes] = (dq_sc[kj] * head ** -0.5).astype(BF16)
        out_ref[:, lanes:lanes + head] = dk_sc[...].astype(BF16)
        out_ref[:, lanes + head:] = dv_sc[...].astype(BF16)

    pairs = part * per_kv * (slots * tokens) ** 2 // 2
    wide = lanes + 2 * head
    kv_block = pl.BlockSpec((None, None, tokens, 2 * head), lambda b, j: (j, b, 0, 0))
    every = pl.BlockSpec((slots, None, tokens, lanes), lambda b, j: (0, b, 0, 0))
    rows = pl.BlockSpec((slots, None, per_kv * 8, tokens), lambda b, j: (0, b, 0, 0))
    return pl.pallas_call(
        body, grid=(part, slots),
        in_specs=[every, kv_block, every, rows, rows],
        out_specs=pl.BlockSpec((None, None, tokens, wide), lambda b, j: (j, b, 0, 0)),
        out_shape=jax.ShapeDtypeStruct((slots, part, tokens, wide), BF16),
        scratch_shapes=[pltpu.VMEM((slots, tokens, lanes), F32), pltpu.VMEM((tokens, head), F32), pltpu.VMEM((tokens, head), F32)],
        compiler_params=params(2), cost_estimate=cost(20 * pairs * head, 12 * q.size), name='attention_bwd',
    )(q, kv, d_o, lse, delta)


def solution(mesh):
    group = mesh.shape['sp']

    def exchange(arr):
        return lax.all_to_all(arr, 'sp', 0, 0, tiled=True)

    def scatter(grad):
        return lax.psum_scatter(grad, 'sp', scatter_dimension=0, tiled=True).astype(BF16)

    def gather(piece):
        return lax.all_gather(piece, 'sp', axis=0, tiled=True)

    def device_step(x_in, dy_in, positions, w_q, w_k, w_v, w_o, w_pre, w_post, q_norm, k_norm):
        head = q_norm.shape[0]
        kv_heads = w_k.shape[1] // head
        rep = group // kv_heads
        assert rep * kv_heads == group and x_in.shape[0] % rep == 0
        assert w_q.shape[1] == 2 * w_k.shape[1]
        w_kv = jnp.concatenate([w_k, w_v], axis=1)
        cosines, sines = rope_tables(positions, head)
        chunks = range(x_in.shape[0] // rep)

        def cut(arr, h):
            return arr[h * rep:(h + 1) * rep]

        def total(pieces):
            return functools.reduce(jnp.add, pieces)

        def mm(expr, left, right):
            return jnp.einsum(expr, left, right, preferred_element_type=F32)

        x_f32 = [cut(x_in, h).astype(F32) for h in chunks]
        normed, pre_pull, kv_proj, q_proj, kv_all, q_all = [], [], [], [], [], []
        for h in chunks:
            value, pull = jax.vjp(pre_norm, x_f32[h], w_pre)
            normed.append(value)
            pre_pull.append(pull)
            kv_proj.append(mm('bsd,dn->bsn', value, w_kv).astype(BF16))
            kv_all.append(exchange(kv_pack(kv_proj[h], k_norm, cosines, sines, head, kv_heads, rep)))
            q_proj.append(mm('bsd,dn->bsn', value, w_q).astype(BF16))
            q_all.append(exchange(q_pack(q_proj[h], q_norm, cosines, sines, head, kv_heads, rep)))
        fwd = [attention_fwd(q_all[h], kv_all[h], head) for h in chunks]
        y_out, dy_f32, d_oall, dw_o, dw_post = [], [], [], [], []
        for h in chunks:
            o_flat = unpack(exchange(fwd[h][0]), kv_heads, rep)
            proj = mm('bsn,nd->bsd', o_flat, w_o).astype(BF16)
            post, post_pull = jax.vjp(post_norm, proj, w_post)
            y_out.append((x_f32[h] + post).astype(BF16))
            dy_f32.append(cut(dy_in, h).astype(F32))
            d_proj, piece = post_pull(dy_f32[h])
            dw_post.append(piece)
            d_oall.append(exchange(pack(mm('bsd,nd->bsn', d_proj, w_o).astype(BF16), kv_heads, rep)))
            dw_o.append(mm('bsn,bsd->nd', o_flat, d_proj))
        dw_o = scatter(total(dw_o))
        d_all = []
        for h in chunks:
            if h == chunks[-1]:
                (d_oall[h], dw_o, *d_all) = lax.optimization_barrier((d_oall[h], dw_o, *d_all))
                dw_o = gather(dw_o)
            delta = row_dots(fwd[h][0], d_oall[h], head)
            d_all.append(attention_bwd(q_all[h], kv_all[h], d_oall[h], fwd[h][1], delta, head))
        d_all = [exchange(arr) for arr in d_all]
        dkv_parts, dq_parts, d_normed, dk_norm, dq_norm = [], [], [], [], []
        for h in chunks:
            if h == chunks[-1] and h > 0:
                d_all[h], dw_o, dkv_parts[-1], dq_parts[-1], d_normed[-1] = lax.optimization_barrier(
                    (d_all[h], dw_o, dkv_parts[-1], dq_parts[-1], d_normed[-1]))
            dk, dv, piece = kv_unpack(d_all[h], kv_proj[h], k_norm, cosines, sines, head, kv_heads, rep)
            dkv = jnp.concatenate([dk, dv], axis=-1)
            dk_norm.append(piece)
            dkv_parts.append(mm('bsd,bsn->dn', normed[h], dkv))
            dq, piece = q_unpack(d_all[h], q_proj[h], q_norm, cosines, sines, head, kv_heads, rep)
            dq_norm.append(piece)
            dq_parts.append(mm('bsd,bsn->dn', normed[h], dq))
            d_normed.append((mm('bsn,dn->bsd', dq, w_q) + mm('bsn,dn->bsd', dkv, w_kv)).astype(BF16))
        dw_kv = gather(scatter(total(dkv_parts)))
        dw_q = gather(scatter(total(dq_parts)))
        dx_out, dw_pre = [], []
        for h in chunks:
            dx_norm, piece = pre_pull[h](d_normed[h])
            dw_pre.append(piece)
            dx_out.append((dy_f32[h] + dx_norm).astype(BF16))
        y_out, dx_out = jnp.concatenate(y_out, axis=0), jnp.concatenate(dx_out, axis=0)
        dw_pre, dw_post, dq_norm, dk_norm = total(dw_pre), total(dw_post), total(dq_norm), total(dk_norm)
        small = lax.psum((dw_pre, dw_post, dq_norm.reshape(head), dk_norm.reshape(head)), 'sp')
        half = w_k.shape[1]
        return (y_out, dx_out, dw_q, dw_kv[:, :half], dw_kv[:, half:], dw_o, *small)

    token_spec = P('dp', 'sp', None)
    return jax.shard_map(device_step, mesh=mesh,
                         in_specs=(token_spec, token_spec, P(('dp', 'sp')), P(None, None), P(None, None), P(None, None), P(None, None), P(None), P(None), P(None), P(None)),
                         out_specs=(token_spec, token_spec, P('dp', None), P('dp', None), P('dp', None), P('dp', None), P('dp'), P('dp'), P('dp'), P('dp')),
                         check_vma=False)
```

time: 2310 us -> 1330 us (0.58)
  blocking collectives: 565 us -> 25.9 us
  matrix products: 749 us -> 302 us
  Pallas kernels: 0 us -> 412 us
  other arithmetic: 404 us -> 62.1 us
  local copies, waits for them, and re-layouts: 283 us -> 32.7 us
  waiting for transfers between devices: 247 us -> 420 us
    psum x1, blocking collectives: 565 us -> 25.9 us  [device_step(): lax.psum((dw_pre, dw_post, dq_norm.reshape(head), dk_norm.reshape(head)),...]
    dot_general x36 -> x18, matrix products: 749 us -> 302 us  [mm(): return jnp.einsum(expr, left, right, preferred_element_type=F32)]
    pallas_call x0 -> x18, Pallas kernels: none -> 412 us  [the longest x2 173 us: attention_fwd(): pl.pallas_call(body, grid=(part, slots), in_specs=[pl.BlockSpec((None, No...]
    reduce_scatter x0 -> x3, waiting for transfers between devices: none -> 171 us  [scatter(): lax.psum_scatter(grad, 'sp', scatter_dimension=0, tiled=True).astype(BF16)]
    another operation x6 -> x0, other arithmetic: 143 us -> none
    reduce_sum x9 -> x0, other arithmetic: 128 us -> none  [the longest x4 61.8 us: attention_fwd(): row_sum = jnp.sum(exp_scores, axis=-1, keepdims=True)]
    reshape x6 -> x0, local copies, waits for them, and re-layouts: 63.8 us -> none  [the longest x2 15.3 us: device_step(): jnp.einsum('bsd,dn->bsn', normed, w_v, preferred_element_type=jnp.float32)]
    convert_element_type x6 -> x0, local copies, waits for them, and re-layouts: 63.3 us -> none  [the longest x4 36 us: norm_rope(): normed = rms_scale(heads_bf.astype(jnp.float32), weight)]
  transfers between devices with their start and end apart: 8 -> 16, of which waited for: 6 -> 11; matrix products, arithmetic and copies ran while one was open for 28% -> 19% of each run, Pallas kernels for 0% -> 29%
where the time goes in v1:
time: 1330 us; the launch traced here: 1320 us
  waiting for transfers between devices  420 us (32%)
  Pallas kernels  412 us (31%)
  matrix products  302 us (23%)
  other arithmetic  62.1 us (5%)
  starting transfers between devices  50 us (4%)
  local copies, waits for them, and re-layouts  32.7 us (2%)
  blocking collectives  25.9 us (2%)
  between operations  14.9 us (1%)
    dot_general x18, matrix products, mm(): return jnp.einsum(expr, left, right, preferred_element_type=F32)  302 us
    all_to_all x10, waiting for transfers between devices, exchange(): return lax.all_to_all(arr, 'sp', 0, 0, tiled=True)  239 us
    pallas_call x2, Pallas kernels, attention_fwd(): pl.pallas_call(body, grid=(part, slots), in_specs=[pl.BlockSpec((None, No...  173 us
    reduce_scatter x3, waiting for transfers between devices, scatter(): lax.psum_scatter(grad, 'sp', scatter_dimension=0, tiled=True).astype(BF16)  171 us
    pallas_call x2, Pallas kernels, attention_bwd(): pl.pallas_call(body, grid=(part, slots), in_specs=[every, kv_block, every...  128 us
    all_to_all x10, starting transfers between devices, exchange(): return lax.all_to_all(arr, 'sp', 0, 0, tiled=True)  49.2 us
  transfers between devices with their start and end apart: 16, of which 11 were waited for; matrix products, arithmetic and copies ran while one was open for 19% of the time, Pallas kernels for 29%

profile of v1, /device:TPU:112, one launch (start us, length us, event | category | flops | bytes accessed | tf_op | source)
XLA Modules:
  0.0 1319.9 jit_solution(7738585415159218219)
XLA Ops:
  8.1 4.9 fusion.22
  15.4 13.8 %fusion.54.x_ref = bf16[2,512,2048]{2,1,0:T(8,128)(2,1)} fusion(bf16[2304,2048]{1,0:T(8,128)(2,1)} %param.14, f32[2304]{0:T(1024)S(1)} %broadcast_add_fusion.1, f32[2,512]{1,0:T(2,128)S(1)} %fusion.66, bf16[4,512,2304]{2,1,0:T(8,128)(2,1)S(1)} %copy-done), kind=kOutput, calls=%fused_computation.88 | convolution fusion | flops 9675210752 | bytes 18366464 | tf_op jit(solution)/shard_map/bsd,dn->bsn/dot_general | solution.py:364
  29.3 8.1 q_pack.2
  37.4 5.3 all-to-all-start
  42.7 15.5 %convolution_convert_fusion.k_ref.v_ref.x_ref = bf16[2,512,2048]{2,1,0:T(8,128)(2,1)} fusion(f32[2,512]{1,0:T(2,128)S(1)} %fusion.68, f32[2304]{0:T(1024)S(1)} %broadcast_add_fusion.1, bf16[4,512,2304]{2,1,0:T(8,128)(2,1)} %param.11, bf16[2304,1024]{1,0:T(8,128)(2,1)} %param.16, bf16[2304,1024]{1,0:T(8,128)(2,1)} %param.15), kind=kOutput, calls=%fused_computation.92 | convolution fusion | flops 9694085120 | bytes 18363392 | tf_op jit(solution)/shard_map/bsd,dn->bsn/dot_general | solution.py:364
  58.2 7.4 kv_pack.3
  65.6 26.7 %all-to-all-done.q_ref = bf16[8,1,512,512]{3,2,1,0:T(8,128)(2,1)} async-done(((bf16[8,1,512,512]{3,2,1,0:T(8,128)(2,1)}), bf16[8,1,512,512]{3,2,1,0:T(8,128)(2,1)}, u32[]{:S(2)}, u32[]{:S(2)}) %all-to-all-start) | async-done | bytes 4194336 | tf_op jit(solution)/shard_map/all_to_all | solution.py:339
  92.3 4.9 all-to-all-start.4
  97.3 15.4 %fusion.57.x_ref = bf16[2,512,2048]{2,1,0:T(8,128)(2,1)} fusion(bf16[2304,2048]{1,0:T(8,128)(2,1)} %param.14, f32[2,512]{1,0:T(2,128)S(1)} %fusion.68, f32[2304]{0:T(1024)S(1)} %broadcast_add_fusion.1, bf16[4,512,2304]{2,1,0:T(8,128)(2,1)} %param.11), kind=kOutput, calls=%fused_computation.89 | convolution fusion | flops 9675210752 | bytes 18363392 | tf_op jit(solution)/shard_map/bsd,dn->bsn/dot_general | solution.py:364
  112.6 8.1 q_pack.3
  120.7 26.0 %all-to-all-done.4.kv_ref = bf16[8,1,512,512]{3,2,1,0:T(8,128)(2,1)} async-done(((bf16[8,1,512,512]{3,2,1,0:T(8,128)(2,1)}), bf16[8,1,512,512]{3,2,1,0:T(8,128)(2,1)}, u32[]{:S(2)}, u32[]{:S(2)}) %all-to-all-start.4) | async-done | bytes 4194336 | tf_op jit(solution)/shard_map/all_to_all | solution.py:339
  151.5 15.5 %convolution_convert_fusion.1.k_ref.v_ref.x_ref = bf16[2,512,2048]{2,1,0:T(8,128)(2,1)} fusion(f32[2304]{0:T(1024)S(1)} %broadcast_add_fusion.1, f32[2,512]{1,0:T(2,128)S(1)} %fusion.66, bf16[4,512,2304]{2,1,0:T(8,128)(2,1)} %param.11, bf16[2304,1024]{1,0:T(8,128)(2,1)} %param.16, bf16[2304,1024]{1,0:T(8,128)(2,1)} %param.15), kind=kOutput, calls=%fused_computation.93 | convolution fusion | flops 9694085120 | bytes 18363392 | tf_op jit(solution)/shard_map/bsd,dn->bsn/dot_general | solution.py:364
  166.9 7.4 kv_pack.2
  174.4 26.5 %all-to-all-done.3.q_ref = bf16[8,1,512,512]{3,2,1,0:T(8,128)(2,1)} async-done(((bf16[8,1,512,512]{3,2,1,0:T(8,128)(2,1)}), bf16[8,1,512,512]{3,2,1,0:T(8,128)(2,1)}, u32[]{:S(2)}, u32[]{:S(2)}) %all-to-all-start.3) | async-done | bytes 4194336 | tf_op jit(solution)/shard_map/all_to_all | solution.py:339
  200.9 5.0 all-to-all-start.1
  205.8 86.7 %attention_fwd.3 = (bf16[8,1,512,512]{3,2,1,0:T(8,128)(2,1)}, f32[8,1,16,512]{3,2,1,0:T(8,128)}) custom-call(bf16[8,1,512,512]{3,2,1,0:T(8,128)(2,1)} %all-to-all-done.3.q_ref, bf16[8,1,512,512]{3,2,1,0:T(8,128)(2,1)} %all-to-all-done.4.kv_ref), custom_call_target="tpu_custom_call" | custom-call | flops 34359738368 | bytes 16777216 | tf_op jit(solution)/shard_map/attention_fwd/pallas_call | solution.py:246
  292.6 4.7 all-to-all-start.5
  297.3 86.7 %attention_fwd.2 = (bf16[8,1,512,512]{3,2,1,0:T(8,128)(2,1)}, f32[8,1,16,512]{3,2,1,0:T(8,128)}) custom-call(bf16[8,1,512,512]{3,2,1,0:T(8,128)(2,1)} %all-to-all-done.q_ref, bf16[8,1,512,512]{3,2,1,0:T(8,128)(2,1)} %all-to-all-done.1.kv_ref), custom_call_target="tpu_custom_call" | custom-call | flops 34359738368 | bytes 16777216 | tf_op jit(solution)/shard_map/attention_fwd/pallas_call | solution.py:246
  384.0 4.8 all-to-all-start.2
  389.3 6.7 unpack.3
  396.1 16.0 %fusion.20 = (f32[2,512]{1,0:T(2,128)S(1)}, bf16[2,512,2304]{2,1,0:T(8,128)(2,1)}) fusion(bf16[2,512,2048]{2,1,0:T(8,128)(2,1)} %unpack.3, bf16[2048,2304]{1,0:T(8,128)(2,1)} %param.17), kind=kOutput, calls=%fused_computation.57 | convolution fusion | flops 9673112576 | bytes 18354176 | tf_op jit(solution)/shard_map/bsn,nd->bsd/dot_general | solution.py:364
  412.0 26.4 %all-to-all-done.2.i_ref = bf16[8,1,512,512]{3,2,1,0:T(8,128)(2,1)} async-done(((bf16[8,1,512,512]{3,2,1,0:T(8,128)(2,1)}), bf16[8,1,512,512]{3,2,1,0:T(8,128)(2,1)}, u32[]{:S(2)}, u32[]{:S(2)}) %all-to-all-start.2) | async-done | bytes 4194336 | tf_op jit(solution)/shard_map/all_to_all | solution.py:339
  438.5 7.6 unpack.2
  446.1 13.8 %fusion.18 = (f32[2,512]{1,0:T(2,128)S(1)}, bf16[2,512,2304]{2,1,0:T(8,128)(2,1)S(1)}) fusion(bf16[2,512,2048]{2,1,0:T(8,128)(2,1)} %unpack.2, bf16[2048,2304]{1,0:T(8,128)(2,1)} %param.17), kind=kOutput, calls=%fused_computation.55 | convolution fusion | flops 9673112576 | bytes 18354176 | tf_op jit(solution)/shard_map/bsn,nd->bsd/dot_general | solution.py:364
  460.0 20.5 %fusion.23 = (bf16[2,512,2304]{2,1,0:T(8,128)(2,1)}, bf16[2,512,2304]{2,1,0:T(8,128)(2,1)}, f32[2304]{0:T(1024)}, f32[2,512]{1,0:T(2,128)S(1)}, f32[2,512]{1,0:T(2,128)S(1)}, /*index=5*/f32[2304]{0:T(1024)}) fusion(bf16[2,512,2304]{2,1,0:T(8,128)(2,1)S(1)} %get-tuple-element.85, f32[2304]{0:T(1024)S(1)} %broadcast_add_fusion, f32[2,512]{1,0:T(2,128)S(1)} %fusion.67, ...), kind=kLoop, calls=%fused_computation.60 | loop fusion | flops 56616448 | bytes 37792768 | tf_op jit(solution)/shard_map/convert_element_type | solution.py:382
  480.6 19.6 %fusion.81 = f32[2048,2304,1]{1,0,2:T(8,128)} fusion(bf16[2,512,2048]{2,1,0:T(8,128)(2,1)} %unpack.2, bf16[2,512,2304]{2,1,0:T(8,128)(2,1)} %copy-done.1, f32[2,512]{1,0:T(2,128)S(1)} %multiply_multiply_fusion.2, f32[2304]{0:T(1024)S(1)} %broadcast_add_fusion, f32[2,512]{1,0:T(2,128)S(1)} %fusion.67, bf16[4,512,2304]{2,1,0:T(8,128)(2,1)} %param.12), kind=kOutput, calls=%fused_computation.118 | convolution fusion | flops 9682550784 | bytes 32523264 | tf_op jit(solution)/shard_map/bsn,bsd->nd/dot_general | solution.py:364
  500.2 22.4 %bitcast_add_fusion.2 = f32[2048,2304]{1,0:T(8,128)} fusion(f32[2048,2304,1]{1,0,2:T(8,128)} %fusion.81, bf16[2,512,2048]{2,1,0:T(8,128)(2,1)} %unpack.3, bf16[2,512,2304]{2,1,0:T(8,128)(2,1)} %get-tuple-element.87, f32[2,512]{1,0:T(2,128)S(1)} %multiply_multiply_fusion.3, f32[2,512]{1,0:T(2,128)S(1)} %fusion.69, f32[2304]{0:T(1024)S(1)} %broadcast_add_fusion, ...), kind=kOutput, calls=%fused_computation.2 | convolution fusion | flops 9687269376 | bytes 51397632 | tf_op jit(solution)/shard_map/bsn,bsd->nd/dot_general | solution.py:364
  522.7 17.0 %fusion.63.i_ref = bf16[2,512,2048]{2,1,0:T(8,128)(2,1)} fusion(bf16[2048,2304]{1,0:T(8,128)(2,1)} %param.17, bf16[2,512,2304]{2,1,0:T(8,128)(2,1)} %copy-done.1, f32[2,512]{1,0:T(2,128)S(1)} %multiply_multiply_fusion.2, f32[2304]{0:T(1024)S(1)} %broadcast_add_fusion, f32[2,512]{1,0:T(2,128)S(1)} %fusion.67, bf16[4,512,2304]{2,1,0:T(8,128)(2,1)} %param.12), kind=kOutput, calls=%fused_computation.91 | convolution fusion | flops 9684647936 | bytes 23086080 | tf_op jit(solution)/shard_map/bsd,nd->bsn/dot_general | solution.py:364
  539.7 6.6 pack.3
  546.3 4.7 all-to-all-start.7
  551.0 16.7 %fusion.60.i_ref = bf16[2,512,2048]{2,1,0:T(8,128)(2,1)} fusion(bf16[2048,2304]{1,0:T(8,128)(2,1)} %param.17, bf16[2,512,2304]{2,1,0:T(8,128)(2,1)} %get-tuple-element.87, f32[2,512]{1,0:T(2,128)S(1)} %multiply_multiply_fusion.3, f32[2,512]{1,0:T(2,128)S(1)} %fusion.69, f32[2304]{0:T(1024)S(1)} %broadcast_add_fusion, bf16[4,512,2304]{2,1,0:T(8,128)(2,1)} %param.12), kind=kOutput, calls=%fused_computation.90 | convolution fusion | flops 9684647936 | bytes 23086080 | tf_op jit(solution)/shard_map/bsd,nd->bsn/dot_general | solution.py:364
  567.7 6.6 pack.2
  574.3 48.6 %all-to-all-done.7.d_ref = bf16[8,1,512,512]{3,2,1,0:T(8,128)(2,1)} async-done(((bf16[8,1,512,512]{3,2,1,0:T(8,128)(2,1)}), bf16[8,1,512,512]{3,2,1,0:T(8,128)(2,1)}, u32[]{:S(2)}, u32[]{:S(2)}) %all-to-all-start.7) | async-done | bytes 4194336 | tf_op jit(solution)/shard_map/all_to_all | solution.py:339
  623.0 4.7 all-to-all-start.6
  627.8 8.0 row_dots.2.delta_ref
  635.8 64.1 %attention_bwd.2 = bf16[8,1,512,1024]{3,2,1,0:T(8,128)(2,1)} custom-call(bf16[8,1,512,512]{3,2,1,0:T(8,128)(2,1)} %all-to-all-done.q_ref, bf16[8,1,512,512]{3,2,1,0:T(8,128)(2,1)} %all-to-all-done.1.kv_ref, bf16[8,1,512,512]{3,2,1,0:T(8,128)(2,1)} %all-to-all-done.7.d_ref, f32[8,1,16,512]{3,2,1,0:T(8,128)} %get-tuple-element.34.lse_ref, ...), custom_call_target="tpu_custom_call" | custom-call | flops 85899345920 | bytes 25165824 | tf_op jit(solution)/shard_map/attention_bwd/pallas_call | solution.py:325
  699.9 10.4 reduce-scatter.4.cloned.1.call-done
  713.1 7.6 row_dots.3.delta_ref
  720.8 5.2 all-to-all-start.9
  725.9 64.1 %attention_bwd.3 = bf16[8,1,512,1024]{3,2,1,0:T(8,128)(2,1)} custom-call(bf16[8,1,512,512]{3,2,1,0:T(8,128)(2,1)} %all-to-all-done.3.q_ref, bf16[8,1,512,512]{3,2,1,0:T(8,128)(2,1)} %all-to-all-done.4.kv_ref, bf16[8,1,512,512]{3,2,1,0:T(8,128)(2,1)} %all-to-all-done.6.d_ref, f32[8,1,16,512]{3,2,1,0:T(8,128)} %get-tuple-element.36.lse_ref, ...), custom_call_target="tpu_custom_call" | custom-call | flops 85899345920 | bytes 25165824 | tf_op jit(solution)/shard_map/attention_bwd/pallas_call | solution.py:325
  790.1 68.2 %all-to-all-done.9.d_ref = bf16[8,1,512,1024]{3,2,1,0:T(8,128)(2,1)} async-done(((bf16[8,1,512,1024]{3,2,1,0:T(8,128)(2,1)}), bf16[8,1,512,1024]{3,2,1,0:T(8,128)(2,1)}, u32[]{:S(2)}, u32[]{:S(2)}) %all-to-all-start.9) | async-done | bytes 8388640 | tf_op jit(solution)/shard_map/all_to_all | solution.py:339
  858.2 5.1 all-to-all-start.8
  863.4 8.1 kv_unpack.2
  871.6 9.9 q_unpack.2
  882.0 14.2 %fusion.79 = f32[2,512,2304]{2,1,0:T(8,128)} fusion(bf16[2,512,2048]{2,1,0:T(8,128)(2,1)S(1)} %constant_dynamic-update-slice_fusion, bf16[2304,1024]{1,0:T(8,128)(2,1)} %param.16, bf16[2304,1024]{1,0:T(8,128)(2,1)} %param.15), kind=kOutput, calls=%fused_computation.117 | convolution fusion | flops 9682550784 | bytes 23068672 | tf_op jit(solution)/shard_map/bsn,dn->bsd/dot_general | solution.py:364
  896.2 13.8 %convolution_bitcast_fusion.1 = f32[2304,2048]{1,0:T(8,128)} fusion(bf16[2,512,2048]{2,1,0:T(8,128)(2,1)S(1)} %constant_dynamic-update-slice_fusion, f32[2304]{0:T(1024)S(1)} %copy-done.7, f32[2,512]{1,0:T(2,128)S(1)} %copy-done.15, bf16[4,512,2304]{2,1,0:T(8,128)(2,1)S(1)} %bitcast.77), kind=kOutput, calls=%fused_computation.32 | convolution fusion | flops 9673113600 | bytes 27803648 | tf_op jit(solution)/shard_map/bsd,bsn->dn/dot_general | solution.py:364
  910.0 13.9 %convolution_bitcast_fusion = f32[2304,2048]{1,0:T(8,128)} fusion(bf16[2,512,2048]{2,1,0:T(8,128)(2,1)S(1)} %copy-done.24, f32[2304]{0:T(1024)S(1)} %copy-done.7, f32[2,512]{1,0:T(2,128)S(1)} %copy-done.15, bf16[4,512,2304]{2,1,0:T(8,128)(2,1)S(1)} %bitcast.77), kind=kOutput, calls=%fused_computation.31 | convolution fusion | flops 9673113600 | bytes 27803648 | tf_op jit(solution)/shard_map/bsd,bsn->dn/dot_general | solution.py:364
  923.9 17.5 %add_convert_fusion.1 = bf16[2,512,2304]{2,1,0:T(8,128)(2,1)} fusion(f32[2,512,2304]{2,1,0:T(8,128)} %fusion.79, bf16[2,512,2048]{2,1,0:T(8,128)(2,1)} %get-tuple-element.41, bf16[2304,2048]{1,0:T(8,128)(2,1)} %param.14), kind=kOutput, calls=%fused_computation.85 | convolution fusion | flops 9668395008 | bytes 27787264 | tf_op jit(solution)/shard_map/bsn,dn->bsd/dot_general | solution.py:364
  941.4 16.4 %all-to-all-done.8.d_ref = bf16[8,1,512,1024]{3,2,1,0:T(8,128)(2,1)} async-done(((bf16[8,1,512,1024]{3,2,1,0:T(8,128)(2,1)}), bf16[8,1,512,1024]{3,2,1,0:T(8,128)(2,1)}, u32[]{:S(2)}, u32[]{:S(2)}) %all-to-all-start.8) | async-done | bytes 8388640 | tf_op jit(solution)/shard_map/all_to_all | solution.py:339
  957.8 9.7 q_unpack.3
  967.5 19.8 %bitcast_add_fusion.1 = f32[2304,2048]{1,0:T(8,128)} fusion(f32[2304,2048]{1,0:T(8,128)} %convolution_bitcast_fusion, bf16[2,512,2048]{2,1,0:T(8,128)(2,1)} %get-tuple-element.44, f32[2,512]{1,0:T(2,128)S(1)} %copy-done.17, f32[2304]{0:T(1024)S(1)} %copy-done.7, bf16[4,512,2304]{2,1,0:T(8,128)(2,1)} %param.11), kind=kOutput, calls=%fused_computation.1 | convolution fusion | flops 9677832192 | bytes 46674944 | tf_op jit(solution)/shard_map/bsd,bsn->dn/dot_general | solution.py:364
  987.4 8.4 kv_unpack.3
  1001.3 19.3 %bitcast_add_fusion = f32[2304,2048]{1,0:T(8,128)} fusion(f32[2304,2048]{1,0:T(8,128)} %convolution_bitcast_fusion.1, bf16[2,512,2048]{2,1,0:T(8,128)(2,1)S(1)} %constant_dynamic-update-slice_fusion.2, f32[2,512]{1,0:T(2,128)S(1)} %copy-done.17, f32[2304]{0:T(1024)S(1)} %copy-done.7, bf16[4,512,2304]{2,1,0:T(8,128)(2,1)} %param.11), kind=kOutput, calls=%fused_computation | convolution fusion | flops 9677832192 | bytes 46674944 | tf_op jit(solution)/shard_map/bsd,bsn->dn/dot_general | solution.py:364
  1020.8 63.6 %reduce-scatter.6.cloned.1.call-done = f32[288,2048]{1,0:T(8,128)} async-done(((f32[2304,2048]{1,0:T(8,128)}), f32[288,2048]{1,0:T(8,128)}) %reduce-scatter.6.cloned.1.call-update) | async-done | bytes 2359312 | tf_op jit(solution)/shard_map/reduce_scatter | solution.py:342
  1087.4 96.5 %reduce-scatter.8.cloned.1.call-done = f32[288,2048]{1,0:T(8,128)} async-done(((f32[2304,2048]{1,0:T(8,128)}), f32[288,2048]{1,0:T(8,128)}) %reduce-scatter.8.cloned.1.call-update) | async-done | bytes 2359312 | tf_op jit(solution)/shard_map/reduce_scatter | solution.py:342
  1187.0 9.4 pad_maximum_fusion
  1196.4 14.2 %fusion.78 = f32[2,512,2304]{2,1,0:T(8,128)} fusion(bf16[2,512,2048]{2,1,0:T(8,128)(2,1)S(1)} %copy-done.5, bf16[2304,1024]{1,0:T(8,128)(2,1)} %param.16, bf16[2304,1024]{1,0:T(8,128)(2,1)} %param.15), kind=kOutput, calls=%fused_computation.116 | convolution fusion | flops 9682550784 | bytes 23068672 | tf_op jit(solution)/shard_map/bsn,dn->bsd/dot_general | solution.py:364
  1210.6 24.0 %fusion.10 = (f32[2304]{0:T(1024)S(1)}, f32[2,512]{1,0:T(2,128)S(1)}, f32[2,512]{1,0:T(2,128)S(1)}, f32[2304]{0:T(1024)S(1)}, bf16[2,512,2304]{2,1,0:T(8,128)(2,1)}) fusion(bf16[2,512,2304]{2,1,0:T(8,128)(2,1)} %add_convert_fusion.1, f32[2,512]{1,0:T(2,128)S(1)} %copy-done.15, bf16[4,512,2304]{2,1,0:T(8,128)(2,1)} %param.11, f32[2304]{0:T(1024)S(1)} %copy-done.7, ...), kind=kOutput, calls=%fused_computation.47 | convolution fusion | flops 9706137600 | bytes 41987072 | tf_op jit(solution)/shard_map/bsn,dn->bsd/dot_general | solution.py:364
  1234.6 25.9 %all-reduce = (f32[2304]{0:T(1024)}, f32[2304]{0:T(1024)}, f32[256]{0:T(256)}, f32[256]{0:T(256)}) all-reduce(f32[2304]{0:T(1024)S(1)} %add.116, f32[2304]{0:T(1024)S(1)} %add.117, f32[256]{0:T(256)S(1)} %bitcast.88, f32[256]{0:T(256)S(1)} %bitcast.89), channel_id=1, replica_groups=mesh['dp'=2,'sp'=8] {'sp'}, use_global_device_ids=true, to_apply=%region_13.0 | all-reduce | flops 5120 | bytes 40960 | tf_op jit(solution)/shard_map/psum | solution.py:419
  1260.6 11.7 fusion.12
  1276.6 10.2 all-gather.8.cloned.1.call-done
  1286.8 8.6 fusion.85
  1295.4 9.4 copy.37
  1304.8 8.0 copy.38
  (111 shorter events, 28.2 us)
Async XLA Ops:
  7.2 8.2 copy-start
  7.2 6.4 copy-start.18
  13.0 0.6 copy-start.10
  13.0 29.7 %copy-start.12 = (f32[2,512]{1,0:T(2,128)}, f32[2,512]{1,0:T(2,128)S(1)}, u32[]{:S(2)}) copy-start(f32[2,512]{1,0:T(2,128)S(1)} %get-tuple-element.67) | copy-start | bytes 12292
  13.6 137.9 %copy-start.14 = (f32[2,512]{1,0:T(2,128)}, f32[2,512]{1,0:T(2,128)S(1)}, u32[]{:S(2)}) copy-start(f32[2,512]{1,0:T(2,128)S(1)} %fusion.66) | copy-start | bytes 12292
  13.6 137.8 %copy-start.6 = (f32[2304]{0:T(1024)}, f32[2304]{0:T(1024)S(1)}, u32[]{:S(2)}) copy-start(f32[2304]{0:T(1024)S(1)} %broadcast_add_fusion.1) | copy-start | bytes 27652
  37.4 55.0 %all-to-all-start = ((bf16[8,1,512,512]{3,2,1,0:T(8,128)(2,1)}), bf16[8,1,512,512]{3,2,1,0:T(8,128)(2,1)}, u32[]{:S(2)}, u32[]{:S(2)}) async-start(bf16[8,1,512,512]{3,2,1,0:T(8,128)(2,1)} %q_pack.2), calls=%async_computation | async-start | bytes 8388608 | tf_op jit(solution)/shard_map/all_to_all | solution.py:339
  42.7 54.5 %copy-start.16 = (f32[2,512]{1,0:T(2,128)}, f32[2,512]{1,0:T(2,128)S(1)}, u32[]{:S(2)}) copy-start(f32[2,512]{1,0:T(2,128)S(1)} %fusion.68) | copy-start | bytes 12292
  92.3 54.4 %all-to-all-start.4 = ((bf16[8,1,512,512]{3,2,1,0:T(8,128)(2,1)}), bf16[8,1,512,512]{3,2,1,0:T(8,128)(2,1)}, u32[]{:S(2)}, u32[]{:S(2)}) async-start(bf16[8,1,512,512]{3,2,1,0:T(8,128)(2,1)} %kv_pack.3), calls=%async_computation.4 | async-start | bytes 8388608 | tf_op jit(solution)/shard_map/all_to_all | solution.py:339
  146.7 54.2 %all-to-all-start.3 = ((bf16[8,1,512,512]{3,2,1,0:T(8,128)(2,1)}), bf16[8,1,512,512]{3,2,1,0:T(8,128)(2,1)}, u32[]{:S(2)}, u32[]{:S(2)}) async-start(bf16[8,1,512,512]{3,2,1,0:T(8,128)(2,1)} %q_pack.3), calls=%async_computation.3 | async-start | bytes 8388608 | tf_op jit(solution)/shard_map/all_to_all | solution.py:339
  200.9 91.7 %all-to-all-start.1 = ((bf16[8,1,512,512]{3,2,1,0:T(8,128)(2,1)}), bf16[8,1,512,512]{3,2,1,0:T(8,128)(2,1)}, u32[]{:S(2)}, u32[]{:S(2)}) async-start(bf16[8,1,512,512]{3,2,1,0:T(8,128)(2,1)} %kv_pack.2), calls=%async_computation.1 | async-start | bytes 8388608 | tf_op jit(solution)/shard_map/all_to_all | solution.py:339
  292.6 91.4 %all-to-all-start.5 = ((bf16[8,1,512,512]{3,2,1,0:T(8,128)(2,1)}), bf16[8,1,512,512]{3,2,1,0:T(8,128)(2,1)}, u32[]{:S(2)}, u32[]{:S(2)}) async-start(bf16[8,1,512,512]{3,2,1,0:T(8,128)(2,1)} %get-tuple-element.33.o_ref), calls=%async_computation.5 | async-start | bytes 8388608 | tf_op jit(solution)/shard_map/all_to_all | solution.py:339
  297.3 92.0 %copy-start.19 = (f32[2304]{0:T(1024)S(1)}, f32[2304]{0:T(1024)}, u32[]{:S(2)}) copy-start(f32[2304]{0:T(1024)} %param.19) | copy-start | bytes 27652
  384.0 54.5 %all-to-all-start.2 = ((bf16[8,1,512,512]{3,2,1,0:T(8,128)(2,1)}), bf16[8,1,512,512]{3,2,1,0:T(8,128)(2,1)}, u32[]{:S(2)}, u32[]{:S(2)}) async-start(bf16[8,1,512,512]{3,2,1,0:T(8,128)(2,1)} %get-tuple-element.32.o_ref), calls=%async_computation.2 | async-start | bytes 8388608 | tf_op jit(solution)/shard_map/all_to_all | solution.py:339
  388.8 321.4 %reduce-scatter.4.cloned.1.call-start = ((), (), s32[]{:S(2)}) async-start(), calls=%async_computation.13 | async-start | bytes 21233664 | tf_op jit(solution)/shard_map/reduce_scatter | solution.py:342
  438.5 21.5 %slice-start = ((s8[9437184]{0:T(1024)(128)(4,1)}), s8[1048576]{0:T(1024)(128)(4,1)S(1)}, s32[]{:S(2)}) async-start(s8[9437184]{0:T(1024)(128)(4,1)} %bitcast.74), calls=%async_computation.19 | async-start | bytes 2097152
  438.5 21.5 %slice-start.6 = ((s8[4718592]{0:T(1024)(128)(4,1)}), s8[4194304]{0:T(1024)(128)(4,1)S(1)}, s32[]{:S(2)}) async-start(s8[4718592]{0:T(1024)(128)(4,1)} %bitcast.78), calls=%async_computation.25 | async-start | bytes 8388608
  446.1 13.9 %slice-start.1 = ((s8[9437184]{0:T(1024)(128)(4,1)}), s8[4194304]{0:T(1024)(128)(4,1)S(1)}, s32[]{:S(2)}) async-start(s8[9437184]{0:T(1024)(128)(4,1)} %bitcast.74), calls=%async_computation.20 | async-start | bytes 8388608
  446.1 13.9 %slice-start.2 = ((s8[9437184]{0:T(1024)(128)(4,1)}), s8[4194304]{0:T(1024)(128)(4,1)S(1)}, s32[]{:S(2)}) async-start(s8[9437184]{0:T(1024)(128)(4,1)} %bitcast.74), calls=%async_computation.21 | async-start | bytes 8388608
  446.1 13.9 %slice-start.7 = ((s8[4718592]{0:T(1024)(128)(4,1)}), s8[524288]{0:T(1024)(128)(4,1)S(1)}, s32[]{:S(2)}) async-start(s8[4718592]{0:T(1024)(128)(4,1)} %bitcast.78), calls=%async_computation.26 | async-start | bytes 1048576
  459.9 20.6 %copy-start.1 = (bf16[2,512,2304]{2,1,0:T(8,128)(2,1)}, bf16[2,512,2304]{2,1,0:T(8,128)(2,1)S(1)}, u32[]{:S(2)}) copy-start(bf16[2,512,2304]{2,1,0:T(8,128)(2,1)S(1)} %get-tuple-element.85) | copy-start | bytes 14155780
  546.3 76.7 %all-to-all-start.7 = ((bf16[8,1,512,512]{3,2,1,0:T(8,128)(2,1)}), bf16[8,1,512,512]{3,2,1,0:T(8,128)(2,1)}, u32[]{:S(2)}, u32[]{:S(2)}) async-start(bf16[8,1,512,512]{3,2,1,0:T(8,128)(2,1)} %pack.3), calls=%async_computation.8 | async-start | bytes 8388608 | tf_op jit(solution)/shard_map/all_to_all | solution.py:339
  623.0 90.1 %all-to-all-start.6 = ((bf16[8,1,512,512]{3,2,1,0:T(8,128)(2,1)}), bf16[8,1,512,512]{3,2,1,0:T(8,128)(2,1)}, u32[]{:S(2)}, u32[]{:S(2)}) async-start(bf16[8,1,512,512]{3,2,1,0:T(8,128)(2,1)} %pack.2), calls=%async_computation.6 | async-start | bytes 8388608 | tf_op jit(solution)/shard_map/all_to_all | solution.py:339
  627.7 330.0 %all-gather.4.cloned.1.call-start = ((), (), s32[]{:S(2)}) async-start(), calls=%async_computation.14 | async-start | bytes 10616832 | tf_op jit(solution)/shard_map/all_gather | solution.py:345
  720.8 137.5 %all-to-all-start.9 = ((bf16[8,1,512,1024]{3,2,1,0:T(8,128)(2,1)}), bf16[8,1,512,1024]{3,2,1,0:T(8,128)(2,1)}, u32[]{:S(2)}, u32[]{:S(2)}) async-start(bf16[8,1,512,1024]{3,2,1,0:T(8,128)(2,1)} %attention_bwd.2), calls=%async_computation.10 | async-start | bytes 16777216 | tf_op jit(solution)/shard_map/all_to_all | solution.py:339
  858.2 99.5 %all-to-all-start.8 = ((bf16[8,1,512,1024]{3,2,1,0:T(8,128)(2,1)}), bf16[8,1,512,1024]{3,2,1,0:T(8,128)(2,1)}, u32[]{:S(2)}, u32[]{:S(2)}) async-start(bf16[8,1,512,1024]{3,2,1,0:T(8,128)(2,1)} %attention_bwd.3), calls=%async_computation.9 | async-start | bytes 16777216 | tf_op jit(solution)/shard_map/all_to_all | solution.py:339
  863.4 221.1 %reduce-scatter.6.cloned.1.call-start = ((), (), s32[]{:S(2)}) async-start(), calls=%async_computation.15 | async-start | bytes 21233664 | tf_op jit(solution)/shard_map/reduce_scatter | solution.py:342
  871.6 9.9 copy-start.3
  871.6 10.2 copy-start.2
  881.5 14.7 %slice-start.3 = ((s8[9437184]{0:T(1024)(128)(4,1)}), s8[4194304]{0:T(1024)(128)(4,1)S(1)}, s32[]{:S(2)}) async-start(s8[9437184]{0:T(1024)(128)(4,1)} %bitcast.76), calls=%async_computation.22 | async-start | bytes 8388608
  882.0 14.2 %slice-start.4 = ((s8[9437184]{0:T(1024)(128)(4,1)}), s8[4194304]{0:T(1024)(128)(4,1)S(1)}, s32[]{:S(2)}) async-start(s8[9437184]{0:T(1024)(128)(4,1)} %bitcast.76), calls=%async_computation.23 | async-start | bytes 8388608
  882.0 14.2 %slice-start.5 = ((s8[9437184]{0:T(1024)(128)(4,1)}), s8[1048576]{0:T(1024)(128)(4,1)S(1)}, s32[]{:S(2)}) async-start(s8[9437184]{0:T(1024)(128)(4,1)} %bitcast.76), calls=%async_computation.24 | async-start | bytes 2097152
  882.0 14.2 %copy-start.7 = (f32[2304]{0:T(1024)S(1)}, f32[2304]{0:T(1024)}, u32[]{:S(2)}) copy-start(f32[2304]{0:T(1024)} %copy-done.6) | copy-start | bytes 27652
  882.0 14.2 %copy-start.15 = (f32[2,512]{1,0:T(2,128)S(1)}, f32[2,512]{1,0:T(2,128)}, u32[]{:S(2)}) copy-start(f32[2,512]{1,0:T(2,128)} %copy-done.14) | copy-start | bytes 12292
  896.2 13.8 %copy-start.24 = (bf16[2,512,2048]{2,1,0:T(8,128)(2,1)S(1)}, bf16[2,512,2048]{2,1,0:T(8,128)(2,1)}, u32[]{:S(2)}) copy-start(bf16[2,512,2048]{2,1,0:T(8,128)(2,1)} %get-tuple-element.41) | copy-start | bytes 12582916
  941.4 26.1 %copy-start.17 = (f32[2,512]{1,0:T(2,128)S(1)}, f32[2,512]{1,0:T(2,128)}, u32[]{:S(2)}) copy-start(f32[2,512]{1,0:T(2,128)} %copy-done.16) | copy-start | bytes 12292
  987.3 196.6 %reduce-scatter.8.cloned.1.call-start = ((), (), s32[]{:S(2)}) async-start(), calls=%async_computation.17 | async-start | bytes 21233664 | tf_op jit(solution)/shard_map/reduce_scatter | solution.py:342
  999.3 2.0 copy-start.4
  1020.7 166.2 %copy-start.8 = (f32[2304]{0:T(1024)S(1)}, f32[2304]{0:T(1024)}, u32[]{:S(2)}) copy-start(f32[2304]{0:T(1024)} %get-tuple-element.76) | copy-start | bytes 27652
  1020.7 166.2 %copy-start.9 = (f32[2304]{0:T(1024)S(1)}, f32[2304]{0:T(1024)}, u32[]{:S(2)}) copy-start(f32[2304]{0:T(1024)} %get-tuple-element.79) | copy-start | bytes 27652
  1020.7 255.9 %all-gather.6.cloned.1.call-start = ((), (), s32[]{:S(2)}) async-start(), calls=%async_computation.16 | async-start | bytes 10616832 | tf_op jit(solution)/shard_map/all_gather | solution.py:345
  1087.3 199.4 %all-gather.8.cloned.1.call-start = ((), (), s32[]{:S(2)}) async-start(), calls=%async_computation.18 | async-start | bytes 10616832 | tf_op jit(solution)/shard_map/all_gather | solution.py:345
  1186.9 9.4 copy-start.21
  1186.9 9.4 copy-start.22
  1186.9 9.4 copy-start.20
  1187.0 9.4 copy-start.23
  1187.0 9.4 copy-start.5
  1210.6 50.0 %copy-start.11 = (f32[2,512]{1,0:T(2,128)S(1)}, f32[2,512]{1,0:T(2,128)}, u32[]{:S(2)}) copy-start(f32[2,512]{1,0:T(2,128)} %copy-done.10) | copy-start | bytes 12292
  1210.6 50.0 %copy-start.13 = (f32[2,512]{1,0:T(2,128)S(1)}, f32[2,512]{1,0:T(2,128)}, u32[]{:S(2)}) copy-start(f32[2,512]{1,0:T(2,128)} %copy-done.12) | copy-start | bytes 12292
Sparse Core Ops, SparseCore 0:
  522.8 187.3 reduce-scatter.3
  720.9 102.2 all-gather.3
  987.4 96.9 reduce-scatter.5
  1086.6 97.2 reduce-scatter.7
  1185.4 49.5 all-gather.5
  1236.4 50.3 all-gather.7
